TPU v7x, 32 devices: a whole 2x2x4 slice. The times are simulated.
32 devices in a mesh: ctx: 16 (over z, y, x), tp: 2 (over core).
Axes of the slice: x: 2, y: 2, z: 4, core: 2. Of those that a mesh axis runs over, the one named last changes fastest.
Arguments:
- byte_states: bfloat16 [4096, 1024], P('ctx'), may hold values from -12 to 12, as said below
- patch_of_byte: int32 [4096], P('ctx'), may hold values from 0 to 125, as said below
- patch_first: int32 [16], replicated, may hold values from 0 to 991, as said below
- moved: int32 [2, 16], replicated, may hold values from 0 to 32, as said below
- w_qkv: bfloat16 [3, 1024, 2048], P(None, None, 'tp'), may hold values from -0.25 to 0.25, as said below
- d_attn: bfloat16 [1024, 2048], P('ctx', 'tp'), may hold values from -6 to 6
Outputs:
- attn_out: bfloat16 [1024, 2048], P('ctx', 'tp')
- byte_grad: bfloat16 [4096, 1024], P('ctx', 'tp')
Inputs may be any that keep to these rules, and one draw needn't show every extreme that they name: `patch_of_byte`: within each byte shard the numbers start at 0 and rise by 0 or 1 from byte to byte; a shard holds at most 126 patches, reached on some shard. `patch_first`: the sum of the patch counts of all earlier byte shards; shard 0 starts at 0. moved[0, 0] = 0 and moved[1, 15] = 0; every other entry is 1 to 32; every patch shard thereby receives exactly 64 patches, and the patch counts agree with patch_first and patch_of_byte. `w_qkv`: independent entries of order 1024 ** -0.5. `byte_states`: entries of order one.
All inputs are finite; a program needn't handle non-finite values.
Results may differ from a plain program's by a relative error of at most 0.011.
Values may be sent and summed in bfloat16 or wider, within the bound.
A program may use at most 64 MiB of HBM per device.

v0:
```python
import functools

import jax
import jax.numpy as jnp
from jax import lax
from jax.experimental import pallas as pl
from jax.experimental.pallas import tpu as pltpu
from jax.sharding import PartitionSpec as P

HD = 128
MESH = pl.DeviceIdType.MESH
VM = pl.BlockSpec(memory_space=pltpu.VMEM)


def remote(src, dst, send, recv, device):
    return pltpu.make_async_remote_copy(
        src_ref=src, dst_ref=dst, send_sem=send, recv_sem=recv, device_id=device, device_id_type=MESH
    )


def whole_kernel(
    n, tp, heads, rows, block,
    bytes_ref, pob_ref, first_ref, moved_ref, w_ref, d_ref,
    attn_ref, grad_ref,
    blk, came, pooled, wbuf, own3, qb, gb, kb, vb, ob, dqb, dkb, dvb, dka, dva,
    o_in, dq_in, dk_in, dv_in, part, own_part, lo_part, hi_part,
    w_sem, send_nb, recv_nb, send_kv, recv_kv, send_qg, recv_qg,
    send_dkv, recv_dkv, send_odq, recv_odq, send_rt, recv_rt, local_sem,
):
    groups = n // heads
    total = n * rows
    half = rows // 2
    scale = HD ** (-0.5)
    bf, f32 = jnp.bfloat16, jnp.float32
    me, mt = lax.axis_index("ctx"), lax.axis_index("tp")
    my_head, my_group = me // groups, lax.rem(me, groups)
    left, right = lax.rem(me + n - 1, n), lax.rem(me + 1, n)
    width = part.shape[2]

    def cols(head):
        return pl.ds(pl.multiple_of(head * HD, HD), HD)

    barrier = pltpu.get_barrier_semaphore()

    def greet(i, carry):
        peer = lax.rem(me + i, n)
        pl.semaphore_signal(barrier, inc=1, device_id=(peer, mt), device_id_type=MESH)
        return carry

    lax.fori_loop(1, n, greet, 0)
    for c in (me, left, right):
        for i in range(1, tp):
            pl.semaphore_signal(
                barrier, inc=1, device_id=(c, lax.rem(mt + i, tp)), device_id_type=MESH
            )
    loads = [pltpu.make_async_copy(w_ref.at[j], wbuf.at[j], w_sem.at[j]) for j in range(3)]
    for j in (1, 2, 0):
        loads[j].start()

    def plan(c):
        below = moved_ref[1, lax.rem(c + n - 1, n)]
        above = moved_ref[0, lax.rem(c + 1, n)]
        start = first_ref[c]
        end = jnp.where(c == n - 1, total, first_ref[lax.rem(c + 1, n)])
        return start, end, below, above, moved_ref[0, c], moved_ref[1, c]

    def numbers(c, rank):
        start, end, below, above, low, high = plan(c)
        return jnp.where(
            rank < below,
            start - below + rank,
            jnp.where(rank >= rows - above, end + rank - (rows - above), start + low + rank - below),
        )

    start, end, below, above, low, high = plan(me)
    count = end - start
    rank = lax.broadcasted_iota(jnp.int32, (2 * rows, 1), 0)
    own_rank = rank - 2 * half
    own_local = jnp.where((own_rank >= below) & (own_rank < rows - above), low + own_rank - below, -1)
    up = jnp.where(rank - half < high, count - high + rank - half, -1)
    wanted = jnp.where(rank < half, rank - half + low, jnp.where(rank < 2 * half, up, own_local))
    pob = pob_ref[...]
    member = (pob == wanted).astype(f32)
    lengths = jnp.maximum(jnp.sum(member, axis=1, keepdims=True), 1.0)
    means = (
        jnp.dot(member.astype(bf), bytes_ref[...], preferred_element_type=f32) / lengths
    ).astype(bf)
    blk[0] = means[:half]
    blk[1] = means[half : 2 * half]
    pl.semaphore_wait(barrier, n - 1 + 3 * (tp - 1))
    near = [
        remote(blk.at[i], came.at[i], send_nb.at[i], recv_nb.at[i], (peer, mt))
        for i, peer in enumerate((left, right))
    ]
    for copy in near:
        copy.start()

    def over_peers(make, wait=False):
        def body(i, carry):
            copy = make(i)
            if wait:
                copy.wait()
            else:
                copy.start()
            return carry

        lax.fori_loop(1, n, body, 0)

    def over_mates(make, wait=False):
        def body(i, carry):
            copy = make(i)
            if wait:
                copy.wait()
            else:
                copy.start()
            return carry

        lax.fori_loop(1, heads, body, 0)

    def to_peer(a, ref, out):
        def make(i):
            peer = lax.rem(me + i, n)
            return remote(
                ref.at[:, cols(peer // groups)], out.at[me], send_kv.at[a, i], recv_kv.at[a, i], (peer, mt)
            )

        return make

    def to_mate(a, ref, out):
        def make(i):
            head = lax.rem(my_head + i, heads)
            return remote(
                ref.at[:, cols(head)], out.at[my_head], send_qg.at[a, i], recv_qg.at[a, i],
                (head * groups + my_group, mt),
            )

        return make

    def back_peer(a, ref, out):
        def make(i):
            peer = lax.rem(me + i, n)
            return remote(
                ref.at[peer], out.at[my_group, :, cols(my_head)], send_dkv.at[a, i], recv_dkv.at[a, i],
                (peer, mt),
            )

        return make

    def back_mate(a, ref, out):
        def make(i):
            head = lax.rem(my_head + i, heads)
            return remote(
                ref.at[head], out.at[:, cols(my_head)], send_odq.at[a, i], recv_odq.at[a, i],
                (head * groups + my_group, mt),
            )

        return make

    mine = cols(my_head)
    send_g = to_mate(0, d_ref, gb)
    send_q = to_mate(1, own3.at[0], qb)
    send_k = to_peer(0, own3.at[1], kb)
    send_v = to_peer(1, own3.at[2], vb)
    over_mates(send_g)
    for copy in near:
        copy.wait()
    pooled[pl.ds(0, half)] = means[2 * half : 3 * half] + came[1]
    pooled[pl.ds(half, half)] = means[3 * half :] + came[0]
    for j, send in ((1, lambda: over_peers(send_k)), (2, lambda: over_peers(send_v)), (0, lambda: over_mates(send_q))):
        loads[j].wait()
        own3[j] = jnp.dot(pooled[...], wbuf[j], preferred_element_type=f32).astype(bf)
        send()
    own = [
        pltpu.make_async_copy(src, dst, local_sem.at[i])
        for i, (src, dst) in enumerate((
            (own3.at[1, :, mine], kb.at[me]), (own3.at[2, :, mine], vb.at[me]),
            (d_ref.at[:, mine], gb.at[my_head]), (own3.at[0, :, mine], qb.at[my_head]),
        ))
    ]
    for copy in own:
        copy.start()
    dka[...] = jnp.zeros_like(dka)
    dva[...] = jnp.zeros_like(dva)
    lane = lax.broadcasted_iota(jnp.int32, (1, total), 1)

    def number_keys(c, ids):
        return jnp.where((lane >= c * rows) & (lane < (c + 1) * rows), numbers(c, lane - c * rows), ids)

    kid = lax.fori_loop(0, n, number_keys, jnp.zeros((1, total), jnp.int32))
    for copy in own:
        copy.wait()
    over_mates(send_g, True)
    over_peers(send_k, True)
    over_peers(send_v, True)
    over_mates(send_q, True)

    over_last = (((1,), (1,)), ((), ()))
    over_first = (((0,), (0,)), ((), ()))
    back_o, back_q = back_mate(0, ob, o_in), back_mate(1, dqb, dq_in)
    row = lax.broadcasted_iota(jnp.int32, (rows, 1), 0)
    step_keys = 128 // rows if rows < 128 else 1
    send_dk, send_dv = back_peer(0, dkb, dk_in), back_peer(1, dvb, dv_in)

    def reach_of(b):
        if b < 0:
            return 0
        reach = min(n, (b + 1) * block * groups + 1)
        return min(n, -(-reach // step_keys) * step_keys)

    for b in reversed(range(heads // block)):
        lo = b * block
        reach, settled = reach_of(b), reach_of(b - 1)
        keys = reach * rows
        q = qb[pl.ds(lo, block)].reshape(block * rows, HD)
        g = gb[pl.ds(lo, block)].reshape(block * rows, HD)
        k = kb[pl.ds(0, reach)].reshape(keys, HD)
        v = vb[pl.ds(0, reach)].reshape(keys, HD)
        qid = jnp.concatenate([numbers((lo + j) * groups + my_group, row) for j in range(block)], axis=0)
        allowed = qid >= kid[:, :keys]
        score = lax.dot_general(q, k, over_last, preferred_element_type=f32) * scale
        score = jnp.where(allowed, score, -jnp.inf)
        top = jnp.max(score, axis=1, keepdims=True)
        e = jnp.exp(score - top)
        prob = e * (1.0 / jnp.sum(e, axis=1, keepdims=True))
        probs = prob.astype(bf)
        out = jnp.dot(probs, v, preferred_element_type=f32).astype(bf)
        delta = jnp.sum(g.astype(f32) * out.astype(f32), axis=1, keepdims=True)
        dprob = lax.dot_general(g, v, over_last, preferred_element_type=f32)
        dscore = (prob * (dprob - delta)).astype(bf)
        dq = (jnp.dot(dscore, k, preferred_element_type=f32) * scale).astype(bf)
        ob[pl.ds(lo, block)] = out.reshape(block, rows, HD)
        dqb[pl.ds(lo, block)] = dq.reshape(block, rows, HD)
        dka[pl.ds(0, keys)] += lax.dot_general(dscore, q, over_first, preferred_element_type=f32)
        dva[pl.ds(0, keys)] += lax.dot_general(probs, g, over_first, preferred_element_type=f32)
        for j in range(block):
            i = lax.rem(lo + j - my_head + heads, heads)

            @pl.when(i != 0)
            def _():
                back_o(i).start()
                back_q(i).start()

        if reach > settled:
            span = pl.ds(settled * rows, (reach - settled) * rows)
            shape = (reach - settled, rows, HD)
            dvb[pl.ds(settled, reach - settled)] = dva[span].astype(bf).reshape(shape)
            dkb[pl.ds(settled, reach - settled)] = (dka[span] * scale).astype(bf).reshape(shape)

            def send_back(peer, carry):
                i = lax.rem(peer - me + n, n)

                @pl.when(i != 0)
                def _():
                    send_dv(i).start()
                    send_dk(i).start()

                return carry

            lax.fori_loop(settled, reach, send_back, 0)

    own = [
        pltpu.make_async_copy(src, dst, local_sem.at[i])
        for i, (src, dst) in enumerate((
            (dkb.at[me], dk_in.at[my_group, :, mine]), (dvb.at[me], dv_in.at[my_group, :, mine]),
            (ob.at[my_head], o_in.at[:, mine]), (dqb.at[my_head], dq_in.at[:, mine]),
        ))
    ]
    for copy in own:
        copy.start()
    for copy in own:
        copy.wait()
    over_mates(back_o, True)
    attn_ref[...] = o_in[...]
    over_mates(back_q, True)
    partial = lax.dot_general(dq_in[...], wbuf[0], over_last, preferred_element_type=f32)
    for send, held, j in ((send_dv, dv_in, 2), (send_dk, dk_in, 1)):
        over_peers(send, True)
        summed = held[0].astype(f32)
        for i in range(1, groups):
            summed = summed + held[i].astype(f32)
        partial += lax.dot_general(summed.astype(bf), wbuf[j], over_last, preferred_element_type=f32)
    for t in range(tp):
        part[t] = partial[:, t * width : (t + 1) * width].astype(bf)
    edge_lo, edge_hi = pl.ds(0, half), pl.ds(rows - half, half)
    copies = []
    for i in range(1, tp):
        t = lax.rem(mt + i, tp)
        copies.append((part.at[t], own_part.at[mt], (me, t)))
    for i in range(tp):
        t = lax.rem(mt + i, tp)
        copies.append((part.at[t, edge_lo], hi_part.at[mt], (left, t)))
        copies.append((part.at[t, edge_hi], lo_part.at[mt], (right, t)))
    copies = [
        remote(src, dst, send_rt.at[i], recv_rt.at[i], peer) for i, (src, dst, peer) in enumerate(copies)
    ]
    for copy in copies:
        copy.start()
    kept = pltpu.make_async_copy(part.at[mt], own_part.at[mt], local_sem.at[0])
    kept.start()
    target = jnp.where(
        pob < low,
        half - low + pob,
        jnp.where(pob >= count - high, half + rows + pob - (count - high), half + below + pob - low),
    )
    chooser = (target == lax.broadcasted_iota(jnp.int32, (2 * rows, 1), 0)).astype(f32)
    sizes = jnp.maximum(jnp.sum(chooser, axis=1, keepdims=True), 1.0)
    kept.wait()
    for copy in copies:
        copy.wait()

    def over_tp(ref):
        value = ref[0].astype(f32)
        for i in range(1, tp):
            value = value + ref[i].astype(f32)
        return value

    returned = jnp.concatenate([over_tp(lo_part), over_tp(own_part), over_tp(hi_part)], axis=0)
    shares = (returned.astype(bf).astype(f32) / sizes).astype(bf)
    grad_ref[...] = lax.dot_general(
        chooser.astype(bf), shares, over_first, preferred_element_type=f32
    ).astype(bf)


def shards(byte_states, patch_of_byte, patch_first, moved, w_qkv, d_attn):
    n, tp = lax.axis_size("ctx"), lax.axis_size("tp")
    rows, feats = d_attn.shape
    size, model = byte_states.shape
    heads = feats // HD
    groups = n // heads
    total = n * rows
    half = rows // 2
    width = model // tp
    block = 2 if heads % 2 == 0 else 1
    bf, f32 = jnp.bfloat16, jnp.float32
    dma = pltpu.SemaphoreType.DMA
    smem = pl.BlockSpec(memory_space=pltpu.SMEM)
    return tuple(pl.pallas_call(
        functools.partial(whole_kernel, n, tp, heads, rows, block),
        out_shape=[
            jax.ShapeDtypeStruct((rows, feats), bf),
            jax.ShapeDtypeStruct((size, width), bf),
        ],
        in_specs=[VM, VM, smem, smem, pl.BlockSpec(memory_space=pl.ANY), VM],
        out_specs=[VM] * 2,
        scratch_shapes=[
            pltpu.VMEM((2, half, model), bf), pltpu.VMEM((2, half, model), bf),
            pltpu.VMEM((rows, model), bf), pltpu.VMEM(w_qkv.shape, bf), pltpu.VMEM((3, rows, feats), bf),
            pltpu.VMEM((heads, rows, HD), bf), pltpu.VMEM((heads, rows, HD), bf),
            pltpu.VMEM((n, rows, HD), bf), pltpu.VMEM((n, rows, HD), bf),
            pltpu.VMEM((heads, rows, HD), bf), pltpu.VMEM((heads, rows, HD), bf),
            pltpu.VMEM((n, rows, HD), bf), pltpu.VMEM((n, rows, HD), bf),
            pltpu.VMEM((total, HD), f32), pltpu.VMEM((total, HD), f32),
            pltpu.VMEM((rows, feats), bf), pltpu.VMEM((rows, feats), bf),
            pltpu.VMEM((groups, rows, feats), bf), pltpu.VMEM((groups, rows, feats), bf),
            pltpu.VMEM((tp, rows, width), bf), pltpu.VMEM((tp, rows, width), bf),
            pltpu.VMEM((tp, half, width), bf), pltpu.VMEM((tp, half, width), bf),
            dma((3,)), dma((2,)), dma((2,)), dma((2, n)), dma((2, n)), dma((2, heads)), dma((2, heads)),
            dma((2, n)), dma((2, n)), dma((2, heads)), dma((2, heads)),
            dma((3 * tp - 1,)), dma((3 * tp - 1,)), dma((4,)),
        ],
        compiler_params=pltpu.CompilerParams(
            collective_id=0, has_side_effects=True, vmem_limit_bytes=56 << 20
        ),
        name="whole",
    )(byte_states, patch_of_byte.reshape(1, size), patch_first, moved, w_qkv, d_attn))


def solution(mesh):
    placed = (P("ctx", None), P("ctx"), P(), P(), P(None, None, "tp"), P("ctx", "tp"))
    return jax.shard_map(
        shards,
        mesh=mesh,
        in_specs=placed,
        out_specs=(P("ctx", "tp"), P("ctx", "tp")),
        check_vma=False,
    )
```

profile of v0, /device:TPU:0, one launch (start us, length us, event | category | flops | bytes accessed | tf_op | source)
XLA Modules:
  0.0 60.2 jit_solution(15027224418949451238)
XLA Ops:
  0.6 56.3 %whole.1 = (bf16[64,1024]{1,0:T(8,128)(2,1)}, bf16[256,512]{1,0:T(8,128)(2,1)}) custom-call(bf16[256,1024]{1,0:T(8,128)(2,1)} %bytes_ref.1, s32[1,256]{1,0:T(1,128)} %bitcast.1, s32[16]{0:T(128)} %first_ref.1, s32[2,16]{1,0:T(2,128)} %moved_ref.1, bf16[3,1024,1024]{2,1,0:T(8,128)(2,1)} %w_ref.1, bf16[64,1024]{1,0:T(8,128)(2,1)} %d_ref.1), custom_call_target="tpu_custom_call" | custom-call | tf_op jit(solution)/shard_map/whole/pallas_call | solution.py:337
  56.9 1.6 %copy.10 = bf16[64,1024]{1,0:T(8,128)(2,1)} copy(bf16[64,1024]{1,0:T(8,128)(2,1)} %get-tuple-element.4) | data formatting | bytes 262144
  58.5 1.7 %copy.11 = bf16[256,512]{1,0:T(8,128)(2,1)} copy(bf16[256,512]{1,0:T(8,128)(2,1)} %get-tuple-element.5) | data formatting | bytes 524288
where the time goes:
time: 60.5 us; the launch traced here: 60.2 us
  Pallas kernels  56.3 us (93%)
  local copies, waits for them, and re-layouts  3.24 us (5%)
  between operations  0.64 us (1%)
    pallas_call x1, Pallas kernels, shards(): pl.pallas_call(functools.partial(whole_kernel, n, tp, heads, rows, block)...  56.3 us
    unnamed x2, local copies, waits for them, and re-layouts  3.24 us

commit v1 on v0

--- a/solution.py
+++ b/solution.py
@@ -321,6 +321,16 @@
     ).astype(bf)
 
 
+def emit_kernel(a_ref, g_ref, a_out, g_out, sem):
+    copies = [
+        pltpu.make_async_copy(src, dst, sem.at[i]) for i, (src, dst) in enumerate(((a_ref, a_out), (g_ref, g_out)))
+    ]
+    for copy in copies:
+        copy.start()
+    for copy in copies:
+        copy.wait()
+
+
 def shards(byte_states, patch_of_byte, patch_first, moved, w_qkv, d_attn):
     n, tp = lax.axis_size("ctx"), lax.axis_size("tp")
     rows, feats = d_attn.shape
@@ -334,12 +344,9 @@
     bf, f32 = jnp.bfloat16, jnp.float32
     dma = pltpu.SemaphoreType.DMA
     smem = pl.BlockSpec(memory_space=pltpu.SMEM)
-    return tuple(pl.pallas_call(
+    results = pl.pallas_call(
         functools.partial(whole_kernel, n, tp, heads, rows, block),
-        out_shape=[
-            jax.ShapeDtypeStruct((rows, feats), bf),
-            jax.ShapeDtypeStruct((size, width), bf),
-        ],
+        out_shape=[pltpu.VMEM((rows, feats), bf), pltpu.VMEM((size, width), bf)],
         in_specs=[VM, VM, smem, smem, pl.BlockSpec(memory_space=pl.ANY), VM],
         out_specs=[VM] * 2,
         scratch_shapes=[
@@ -359,10 +366,19 @@
             dma((3 * tp - 1,)), dma((3 * tp - 1,)), dma((4,)),
         ],
         compiler_params=pltpu.CompilerParams(
-            collective_id=0, has_side_effects=True, vmem_limit_bytes=56 << 20
+            collective_id=0, has_side_effects=True, vmem_limit_bytes=60 << 20
         ),
         name="whole",
-    )(byte_states, patch_of_byte.reshape(1, size), patch_first, moved, w_qkv, d_attn))
+    )(byte_states, patch_of_byte.reshape(1, size), patch_first, moved, w_qkv, d_attn)
+    results = [pltpu.with_memory_space_constraint(x, pltpu.VMEM) for x in results]
+    return tuple(pl.pallas_call(
+        emit_kernel,
+        out_shape=[jax.ShapeDtypeStruct((rows, feats), bf), jax.ShapeDtypeStruct((size, width), bf)],
+        in_specs=[VM, VM],
+        out_specs=[pl.BlockSpec(memory_space=pl.ANY)] * 2,
+        scratch_shapes=[dma((2,))],
+        name="emit",
+    )(*results))
 
 
 def solution(mesh):

time: 60.5 us -> 57.3 us (0.947)
  local copies, waits for them, and re-layouts: 3.24 us -> 0 us
    unnamed x2 -> x0, local copies, waits for them, and re-layouts: 3.24 us -> none
    pallas_call x0 -> x1, Pallas kernels: none -> 0.77 us  [shards(): pl.pallas_call(emit_kernel, out_shape=[jax.ShapeDtypeStruct((rows, feats)...]
    pallas_call x1, Pallas kernels: 56.3 us -> 55.6 us  [shards(): pl.pallas_call(functools.partial(whole_kernel, n, tp, heads, rows, block)...]
where the time goes in v1:
time: 57.3 us; the launch traced here: 57 us
  Pallas kernels  56.4 us (98%)
  between operations  0.64 us (1%)
    pallas_call x1, Pallas kernels, shards(): pl.pallas_call(functools.partial(whole_kernel, n, tp, heads, rows, block)...  55.6 us

profile of v1, /device:TPU:0, one launch (start us, length us, event | category | flops | bytes accessed | tf_op | source)
XLA Modules:
  0.0 57.0 jit_solution(17660222060613850951)
XLA Ops:
  0.6 55.6 %whole.1 = (bf16[64,1024]{1,0:T(8,128)(2,1)S(1)}, bf16[256,512]{1,0:T(8,128)(2,1)S(1)}) custom-call(bf16[256,1024]{1,0:T(8,128)(2,1)} %bytes_ref.1, s32[1,256]{1,0:T(1,128)} %bitcast.1, s32[16]{0:T(128)} %first_ref.1, s32[2,16]{1,0:T(2,128)} %moved_ref.1, bf16[3,1024,1024]{2,1,0:T(8,128)(2,1)} %w_ref.1, bf16[64,1024]{1,0:T(8,128)(2,1)} %d_ref.1), custom_call_target="tpu_custom_call" | custom-call | tf_op jit(solution)/shard_map/whole/pallas_call | solution.py:347
  56.2 0.8 %emit.1 = (bf16[64,1024]{1,0:T(8,128)(2,1)}, bf16[256,512]{1,0:T(8,128)(2,1)}) custom-call(bf16[64,1024]{1,0:T(8,128)(2,1)S(1)} %get-tuple-element.4.a_ref, bf16[256,512]{1,0:T(8,128)(2,1)S(1)} %get-tuple-element.5.g_ref), custom_call_target="tpu_custom_call" | custom-call | tf_op jit(solution)/shard_map/emit/pallas_call | solution.py:374

commit v2 on v1

v2 whole, which is shorter than its diff:
```python
import functools

import jax
import jax.numpy as jnp
from jax import lax
from jax.experimental import pallas as pl
from jax.experimental.pallas import tpu as pltpu
from jax.sharding import PartitionSpec as P

HD = 128
MESH = pl.DeviceIdType.MESH
VM = pl.BlockSpec(memory_space=pltpu.VMEM)
ANY = pl.BlockSpec(memory_space=pl.ANY)


def remote(src, dst, send, recv, device):
    return pltpu.make_async_remote_copy(
        src_ref=src, dst_ref=dst, send_sem=send, recv_sem=recv, device_id=device, device_id_type=MESH
    )


def each(lo, hi, act):
    def body(i, carry):
        act(i)
        return carry

    lax.fori_loop(lo, hi, body, 0)


def whole_kernel(
    n, tp, heads, rows, block, per,
    bytes_hbm, pob_hbm, first_hbm, moved_hbm, w_hbm, d_hbm,
    attn_ref, grad_ref,
    bytes_ref, pob_ref, first_ref, moved_ref, wbuf, d_ref,
    blk, came, pooled, own3, qb, gb, kb, vb, ob, dqb, dkb, dvb, xk, xv, dka, dva,
    o_in, dq_in, dk_in, dv_in, part, own_part, lo_part, hi_part,
    in_sem, w_sem, send_nb, recv_nb, send_kv, recv_kv, send_fw, recv_fw, send_qg, recv_qg,
    send_mg, recv_mg, send_dkv, recv_dkv, send_odq, recv_odq, send_rt, recv_rt, local_sem,
):
    pairs = n // 2
    groups = pairs // heads
    stride = 2 * groups
    total = n * rows
    half = rows // 2
    scale = HD ** (-0.5)
    bf, f32 = jnp.bfloat16, jnp.float32
    me, mt = lax.axis_index("ctx"), lax.axis_index("tp")
    sub = lax.rem(mt, 2)
    base = mt - sub
    mate = (me, base + 1 - sub)
    parity, place = lax.rem(me, 2), me // 2
    source_tp = base + parity
    my_head, my_group = place // groups, lax.rem(place, groups)
    offset = 2 * my_group + sub
    slot = me // stride
    left, right = lax.rem(me + n - 1, n), lax.rem(me + 1, n)
    has_left, has_right = me > 0, me < n - 1
    width = part.shape[2]

    def cols(head, count=1):
        return pl.ds(pl.multiple_of(head * HD, HD), count * HD)

    barrier = pltpu.get_barrier_semaphore()

    def greet(i):
        peer = lax.rem(me + i, n)
        for core in range(2):
            pl.semaphore_signal(barrier, inc=1, device_id=(peer, base + core), device_id_type=MESH)

    pl.semaphore_signal(barrier, inc=1, device_id=mate, device_id_type=MESH)
    each(1, n, greet)
    for c in (me, left, right):
        for i in range(2, tp):
            pl.semaphore_signal(
                barrier, inc=1, device_id=(c, lax.rem(base + i, tp)), device_id_type=MESH
            )
    inputs = [
        pltpu.make_async_copy(src, dst, in_sem.at[i])
        for i, (src, dst) in enumerate((
            (pob_hbm, pob_ref), (first_hbm, first_ref), (moved_hbm, moved_ref), (bytes_hbm, bytes_ref),
            (d_hbm, d_ref),
        ))
    ]
    for copy in inputs:
        copy.start()
    loads = [pltpu.make_async_copy(w_hbm.at[j], wbuf.at[j], w_sem.at[j]) for j in range(3)]
    for copy in inputs[:3]:
        copy.wait()

    def plan(c):
        below = moved_ref[1, lax.rem(c + n - 1, n)]
        above = moved_ref[0, lax.rem(c + 1, n)]
        start = first_ref[c]
        end = jnp.where(c == n - 1, total, first_ref[lax.rem(c + 1, n)])
        return start, end, below, above, moved_ref[0, c], moved_ref[1, c]

    def numbers(c, rank):
        start, end, below, above, low, high = plan(c)
        return jnp.where(
            rank < below,
            start - below + rank,
            jnp.where(rank >= rows - above, end + rank - (rows - above), start + low + rank - below),
        )

    start, end, below, above, low, high = plan(me)
    count = end - start
    rank = lax.broadcasted_iota(jnp.int32, (2 * rows, 1), 0)
    own_rank = rank - 2 * half
    own_local = jnp.where((own_rank >= below) & (own_rank < rows - above), low + own_rank - below, -1)
    up = jnp.where(rank - half < high, count - high + rank - half, -1)
    wanted = jnp.where(rank < half, rank - half + low, jnp.where(rank < 2 * half, up, own_local))
    pob = pob_ref[...]
    member = (pob == wanted).astype(f32)
    lengths = jnp.maximum(jnp.sum(member, axis=1, keepdims=True), 1.0)
    inputs[3].wait()
    for j in (1, 0, 2):
        loads[j].start()
    means = (
        jnp.dot(member.astype(bf), bytes_ref[...], preferred_element_type=f32) / lengths
    ).astype(bf)
    blk[0] = means[:half]
    blk[1] = means[half : 2 * half]

    @pl.when(me == 0)
    def _():
        came[1] = jnp.zeros_like(came[1])
        lo_part[...] = jnp.zeros_like(lo_part)

    @pl.when(me == n - 1)
    def _():
        came[0] = jnp.zeros_like(came[0])
        hi_part[...] = jnp.zeros_like(hi_part)

    pl.semaphore_wait(barrier, 2 * n - 1 + 3 * (tp - 2))
    to_left = remote(blk.at[0], came.at[0], send_nb.at[0], recv_nb.at[0], (left, mt))
    to_right = remote(blk.at[1], came.at[1], send_nb.at[1], recv_nb.at[1], (right, mt))
    pl.when(has_left)(to_left.start)
    pl.when(has_right)(to_right.start)

    def send_block(a, ref, out):
        def make(i):
            chip = 2 * i + sub
            return chip, remote(
                ref.at[:, cols(i // groups)], out.at[me], send_kv.at[a, i], recv_kv.at[a, place],
                (chip, base + parity),
            )

        return make

    def send_query(a, ref, out):
        def make(h):
            chip = 2 * (h * groups + my_group) + sub
            return chip, remote(
                ref.at[:, cols(h)], out.at[slot], send_qg.at[a, h], recv_qg.at[a, slot],
                (chip, base + parity),
            )

        return make

    def forward(a, ref, block_at):
        return remote(
            ref.at[block_at], ref.at[block_at], send_fw.at[a, block_at // 2], recv_fw.at[a, block_at // 2], mate
        )

    def back_query(a, ref, out):
        def make(j):
            c = j * stride + offset
            return c, remote(
                ref.at[j], out.at[:, cols(my_head)], send_odq.at[a, j], recv_odq.at[a, my_head], (c, source_tp)
            )

        return make

    def back_block(a, ref, out):
        def make(i):
            c = 2 * i + sub
            return c, remote(
                ref.at[c], out.at[my_group, :, cols(my_head)], send_dkv.at[a, i], recv_dkv.at[a, place],
                (c, source_tp),
            )

        return make

    def start_each(lo, hi, make):
        def act(i):
            other, copy = make(i)
            pl.when(other != me)(copy.start)

        each(lo, hi, act)

    def sent_each(lo, hi, make):
        def act(i):
            other, copy = make(i)
            pl.when(other != me)(copy.wait_send)

        each(lo, hi, act)

    send_g, send_q = send_query(0, d_ref, gb), send_query(1, own3.at[0], qb)
    send_k, send_v = send_block(0, own3.at[1], kb), send_block(1, own3.at[2], vb)
    inputs[4].wait()
    start_each(0, heads, send_g)
    lane = lax.broadcasted_iota(jnp.int32, (1, total), 1)

    def number_keys(c, ids):
        return jnp.where((lane >= c * rows) & (lane < (c + 1) * rows), numbers(c, lane - c * rows), ids)

    kid = lax.fori_loop(0, n, number_keys, jnp.zeros((1, total), jnp.int32))
    dka[...] = jnp.zeros_like(dka)
    dva[...] = jnp.zeros_like(dva)
    pl.when(has_left)(to_right.wait_recv)
    pl.when(has_right)(to_left.wait_recv)
    pooled[pl.ds(0, half)] = means[2 * half : 3 * half] + came[1]
    pooled[pl.ds(half, half)] = means[3 * half :] + came[0]
    chunks = heads // per
    mine = cols(my_head)
    for j, make in ((1, send_k), (0, send_q), (2, send_v)):
        loads[j].wait()
        for s in range(chunks):
            chunk = lax.rem(my_head // per + (chunks + 1) // 2 + s, chunks)
            span = cols(chunk * per, per)
            own3[j, :, span] = jnp.dot(
                pooled[...], wbuf[j, :, span], preferred_element_type=f32
            ).astype(bf)
            each_head = per if j == 0 else per * groups
            start_each(chunk * each_head, (chunk + 1) * each_head, make)

    @pl.when(parity == sub)
    def _():
        qb[slot] = own3[0, :, mine]
        kb[me] = own3[1, :, mine]
        vb[me] = own3[2, :, mine]
        gb[slot] = d_ref[:, mine]

    def take_blocks(a, ref):
        def act(i):
            c = 2 * i + sub
            pl.when(c != me)(remote(
                ref.at[c], ref.at[c], send_kv.at[a, i], recv_kv.at[a, i], (c, source_tp)
            ).wait_recv)
            forward(a, ref, c).start()

        each(0, pairs, act)

    def take_forwards(a, ref):
        each(0, pairs, lambda i: forward(a, ref, 2 * i + 1 - sub).wait_recv())

    def take_queries(a, ref):
        def act(j):
            c = j * stride + offset
            pl.when(c != me)(remote(
                ref.at[j], ref.at[j], send_qg.at[a, j], recv_qg.at[a, j], (c, source_tp)
            ).wait_recv)

        each(0, heads, act)

    take_blocks(0, kb)
    take_queries(1, qb)
    take_forwards(0, kb)
    take_blocks(1, vb)
    take_forwards(1, vb)
    take_queries(0, gb)

    over_last = (((1,), (1,)), ((), ()))
    over_first = (((0,), (0,)), ((), ()))
    back_o, back_q = back_query(0, ob, o_in), back_query(1, dqb, dq_in)
    back_k, back_v = back_block(0, dkb, dk_in), back_block(1, dvb, dv_in)
    row = lax.broadcasted_iota(jnp.int32, (rows, 1), 0)
    step_keys = max(2, 128 // rows)

    def reach_of(b):
        if b < 0:
            return 0
        reach = min(n, (b + 1) * block * stride + 1)
        return min(n, -(-reach // step_keys) * step_keys)

    def at(c):
        return pl.ds(pl.multiple_of(c * rows, rows), rows)

    def hand_over(lo, hi):
        def act(i):
            c = 2 * i + 1 - sub
            for a, (acc, buf, out, factor) in enumerate(((dka, dkb, xk, scale), (dva, dvb, xv, None))):
                value = acc[at(c)]
                buf[c] = (value if factor is None else value * factor).astype(bf)
                remote(buf.at[c], out.at[i], send_mg.at[a, i], recv_mg.at[a, i], mate).start()

        each(lo // 2, hi // 2, act)

    def send_home(lo, hi):
        def act(i):
            c = 2 * i + sub
            for a, (acc, buf, got, factor, make) in enumerate((
                (dka, dkb, xk, scale, back_k), (dva, dvb, xv, None, back_v)
            )):
                remote(buf.at[c], got.at[i], send_mg.at[a, i], recv_mg.at[a, i], mate).wait_recv()
                value = acc[at(c)]
                value = value if factor is None else value * factor
                buf[c] = (value + got[i].astype(f32)).astype(bf)
                pl.when(c != me)(make(i)[1].start)

        each(lo // 2, hi // 2, act)

    late = None
    for b in reversed(range(heads // block)):
        lo = b * block
        reach, settled = reach_of(b), reach_of(b - 1)
        keys = reach * rows
        q = qb[pl.ds(lo, block)].reshape(block * rows, HD)
        g = gb[pl.ds(lo, block)].reshape(block * rows, HD)
        k = kb[pl.ds(0, reach)].reshape(keys, HD)
        v = vb[pl.ds(0, reach)].reshape(keys, HD)
        qid = jnp.concatenate([numbers((lo + j) * stride + offset, row) for j in range(block)], axis=0)
        allowed = qid >= kid[:, :keys]
        score = lax.dot_general(q, k, over_last, preferred_element_type=f32) * scale
        score = jnp.where(allowed, score, -jnp.inf)
        top = jnp.max(score, axis=1, keepdims=True)
        e = jnp.exp(score - top)
        prob = e * (1.0 / jnp.sum(e, axis=1, keepdims=True))
        probs = prob.astype(bf)
        out = jnp.dot(probs, v, preferred_element_type=f32).astype(bf)
        delta = jnp.sum(g.astype(f32) * out.astype(f32), axis=1, keepdims=True)
        dprob = lax.dot_general(g, v, over_last, preferred_element_type=f32)
        dscore = (prob * (dprob - delta)).astype(bf)
        dq = (jnp.dot(dscore, k, preferred_element_type=f32) * scale).astype(bf)
        ob[pl.ds(lo, block)] = out.reshape(block, rows, HD)
        dqb[pl.ds(lo, block)] = dq.reshape(block, rows, HD)
        dka[pl.ds(0, keys)] += lax.dot_general(dscore, q, over_first, preferred_element_type=f32)
        dva[pl.ds(0, keys)] += lax.dot_general(probs, g, over_first, preferred_element_type=f32)
        start_each(lo, lo + block, back_o)
        start_each(lo, lo + block, back_q)
        if reach > settled:
            hand_over(settled, reach)
        if late is not None:
            send_home(*late)
        late = (settled, reach) if reach > settled else None
    if late is not None:
        send_home(*late)

    @pl.when(parity == sub)
    def _():
        o_in[:, mine] = ob[slot]
        dq_in[:, mine] = dqb[slot]
        dk_in[my_group, :, mine] = dkb[me]
        dv_in[my_group, :, mine] = dvb[me]

    def take_back(a, into):
        def act(h):
            chip = 2 * (h * groups + my_group) + sub
            pl.when(chip != me)(remote(
                into.at[:, cols(h)], into.at[:, cols(h)], send_odq.at[a, h], recv_odq.at[a, h],
                (chip, base + parity),
            ).wait_recv)

        each(0, heads, act)

    def take_back_blocks(a, into):
        def act(i):
            chip = 2 * i + sub
            there = into.at[lax.rem(i, groups), :, cols(i // groups)]
            pl.when(chip != me)(remote(
                there, there, send_dkv.at[a, i], recv_dkv.at[a, i], (chip, base + parity)
            ).wait_recv)

        each(0, pairs, act)

    take_back(0, o_in)
    attn_ref[...] = o_in[...]
    take_back(1, dq_in)
    partial = lax.dot_general(dq_in[...], wbuf[0], over_last, preferred_element_type=f32)
    for a, held, j in ((1, dv_in, 2), (0, dk_in, 1)):
        take_back_blocks(a, held)
        summed = held[0]
        if groups > 1:
            summed = summed.astype(f32)
            for i in range(1, groups):
                summed = summed + held[i].astype(f32)
            summed = summed.astype(bf)
        partial += lax.dot_general(summed, wbuf[j], over_last, preferred_element_type=f32)
    for t in range(tp):
        part[t] = partial[:, t * width : (t + 1) * width].astype(bf)
    edge_lo, edge_hi = pl.ds(0, half), pl.ds(rows - half, half)
    copies = []
    for i in range(tp):
        t = lax.rem(mt + i, tp)
        copies.append((has_left, has_right, remote(
            part.at[t, edge_lo], hi_part.at[mt], send_rt.at[0, i], recv_rt.at[0, i], (left, t)
        )))
        copies.append((has_right, has_left, remote(
            part.at[t, edge_hi], lo_part.at[mt], send_rt.at[1, i], recv_rt.at[1, i], (right, t)
        )))
        if i > 0:
            copies.append((None, None, remote(
                part.at[t], own_part.at[mt], send_rt.at[2, i], recv_rt.at[2, i], (me, t)
            )))
    for sends, _, copy in copies:
        copy.start() if sends is None else pl.when(sends)(copy.start)
    own_part[mt] = part[mt]
    target = jnp.where(
        pob < low,
        half - low + pob,
        jnp.where(pob >= count - high, half + rows + pob - (count - high), half + below + pob - low),
    )
    chooser = (target == lax.broadcasted_iota(jnp.int32, (2 * rows, 1), 0)).astype(f32)
    sizes = jnp.maximum(jnp.sum(chooser, axis=1, keepdims=True), 1.0)
    pl.when(has_left)(to_left.wait_send)
    pl.when(has_right)(to_right.wait_send)
    sent_each(0, heads, send_g)
    sent_each(0, heads, send_q)
    sent_each(0, pairs, send_k)
    sent_each(0, pairs, send_v)
    sent_each(0, heads, back_o)
    sent_each(0, heads, back_q)
    sent_each(0, pairs, back_k)
    sent_each(0, pairs, back_v)

    def sent_to_mate(i):
        for a, (ref, acc, got) in enumerate(((kb, dkb, xk), (vb, dvb, xv))):
            forward(a, ref, 2 * i + sub).wait_send()
            remote(acc.at[2 * i], got.at[i], send_mg.at[a, i], recv_mg.at[a, i], mate).wait_send()

    each(0, pairs, sent_to_mate)
    for sends, comes, copy in copies:
        copy.wait_recv() if comes is None else pl.when(comes)(copy.wait_recv)
        copy.wait_send() if sends is None else pl.when(sends)(copy.wait_send)

    def over_tp(ref):
        value = ref[0].astype(f32)
        for i in range(1, tp):
            value = value + ref[i].astype(f32)
        return value

    returned = jnp.concatenate([over_tp(lo_part), over_tp(own_part), over_tp(hi_part)], axis=0)
    shares = (returned.astype(bf).astype(f32) / sizes).astype(bf)
    grad_ref[...] = lax.dot_general(
        chooser.astype(bf), shares, over_first, preferred_element_type=f32
    ).astype(bf)


def emit_kernel(a_ref, g_ref, a_out, g_out, sem):
    copies = [
        pltpu.make_async_copy(src, dst, sem.at[i]) for i, (src, dst) in enumerate(((a_ref, a_out), (g_ref, g_out)))
    ]
    for copy in copies:
        copy.start()
    for copy in copies:
        copy.wait()


def shards(byte_states, patch_of_byte, patch_first, moved, w_qkv, d_attn):
    n, tp = lax.axis_size("ctx"), lax.axis_size("tp")
    rows, feats = d_attn.shape
    size, model = byte_states.shape
    heads = feats // HD
    pairs = n // 2
    groups = pairs // heads
    total = n * rows
    half = rows // 2
    width = model // tp
    block = per = 2 if heads % 2 == 0 else 1
    assert tp % 2 == 0 and n % 2 == 0 and pairs % heads == 0
    bf, f32, i32 = jnp.bfloat16, jnp.float32, jnp.int32
    dma = pltpu.SemaphoreType.DMA
    results = pl.pallas_call(
        functools.partial(whole_kernel, n, tp, heads, rows, block, per),
        out_shape=[pltpu.VMEM((rows, feats), bf), pltpu.VMEM((size, width), bf)],
        in_specs=[ANY] * 6,
        out_specs=[VM] * 2,
        scratch_shapes=[
            pltpu.VMEM((size, model), bf), pltpu.VMEM((1, size), i32),
            pltpu.SMEM((n,), i32), pltpu.SMEM((2, n), i32),
            pltpu.VMEM(w_qkv.shape, bf), pltpu.VMEM((rows, feats), bf),
            pltpu.VMEM((2, half, model), bf), pltpu.VMEM((2, half, model), bf),
            pltpu.VMEM((rows, model), bf), pltpu.VMEM((3, rows, feats), bf),
            pltpu.VMEM((heads, rows, HD), bf), pltpu.VMEM((heads, rows, HD), bf),
            pltpu.VMEM((n, rows, HD), bf), pltpu.VMEM((n, rows, HD), bf),
            pltpu.VMEM((heads, rows, HD), bf), pltpu.VMEM((heads, rows, HD), bf),
            pltpu.VMEM((n, rows, HD), bf), pltpu.VMEM((n, rows, HD), bf),
            pltpu.VMEM((pairs, rows, HD), bf), pltpu.VMEM((pairs, rows, HD), bf),
            pltpu.VMEM((total, HD), f32), pltpu.VMEM((total, HD), f32),
            pltpu.VMEM((rows, feats), bf), pltpu.VMEM((rows, feats), bf),
            pltpu.VMEM((groups, rows, feats), bf), pltpu.VMEM((groups, rows, feats), bf),
            pltpu.VMEM((tp, rows, width), bf), pltpu.VMEM((tp, rows, width), bf),
            pltpu.VMEM((tp, half, width), bf), pltpu.VMEM((tp, half, width), bf),
            dma((5,)), dma((3,)), dma((2,)), dma((2,)), dma((2, pairs)), dma((2, pairs)),
            dma((2, pairs)), dma((2, pairs)), dma((2, heads)), dma((2, heads)),
            dma((2, pairs)), dma((2, pairs)), dma((2, pairs)), dma((2, pairs)),
            dma((2, heads)), dma((2, heads)), dma((3, tp)), dma((3, tp)), dma((4,)),
        ],
        compiler_params=pltpu.CompilerParams(
            collective_id=0, has_side_effects=True, vmem_limit_bytes=60 << 20
        ),
        name="whole",
    )(byte_states, patch_of_byte.reshape(1, size), patch_first, moved, w_qkv, d_attn)
    results = [pltpu.with_memory_space_constraint(x, pltpu.VMEM) for x in results]
    return tuple(pl.pallas_call(
        emit_kernel,
        out_shape=[jax.ShapeDtypeStruct((rows, feats), bf), jax.ShapeDtypeStruct((size, width), bf)],
        in_specs=[VM, VM],
        out_specs=[ANY] * 2,
        scratch_shapes=[dma((2,))],
        name="emit",
    )(*results))


def solution(mesh):
    placed = (P("ctx", None), P("ctx"), P(), P(), P(None, None, "tp"), P("ctx", "tp"))
    return jax.shard_map(
        shards,
        mesh=mesh,
        in_specs=placed,
        out_specs=(P("ctx", "tp"), P("ctx", "tp")),
        check_vma=False,
    )
```

time: 57.3 us -> 50.4 us (0.88)
  Pallas kernels: 56.4 us -> 49.6 us
    pallas_call x1, Pallas kernels: 55.6 us -> 48.8 us  [shards(): pl.pallas_call(functools.partial(whole_kernel, n, tp, heads, rows, block,...]
where the time goes in v2:
time: 50.4 us; the launch traced here: 50.2 us
  Pallas kernels  49.6 us (98%)
  between operations  0.64 us (1%)
    pallas_call x1, Pallas kernels, shards(): pl.pallas_call(functools.partial(whole_kernel, n, tp, heads, rows, block,...  48.8 us

profile of v2, /device:TPU:0, one launch (start us, length us, event | category | flops | bytes accessed | tf_op | source)
XLA Modules:
  0.0 50.2 jit_solution(799454415541872742)
XLA Ops:
  0.6 48.8 %whole.1 = (bf16[64,1024]{1,0:T(8,128)(2,1)S(1)}, bf16[256,512]{1,0:T(8,128)(2,1)S(1)}) custom-call(bf16[256,1024]{1,0:T(8,128)(2,1)} %bytes_hbm.1, s32[1,256]{1,0:T(1,128)} %bitcast.1, s32[16]{0:T(128)} %first_hbm.1, s32[2,16]{1,0:T(2,128)} %moved_hbm.1, bf16[3,1024,1024]{2,1,0:T(8,128)(2,1)} %w_hbm.1, bf16[64,1024]{1,0:T(8,128)(2,1)} %d_hbm.1), custom_call_target="tpu_custom_call" | custom-call | tf_op jit(solution)/shard_map/whole/pallas_call | solution.py:463
  49.4 0.8 %emit.1 = (bf16[64,1024]{1,0:T(8,128)(2,1)}, bf16[256,512]{1,0:T(8,128)(2,1)}) custom-call(bf16[64,1024]{1,0:T(8,128)(2,1)S(1)} %get-tuple-element.4.a_ref, bf16[256,512]{1,0:T(8,128)(2,1)S(1)} %get-tuple-element.5.g_ref), custom_call_target="tpu_custom_call" | custom-call | tf_op jit(solution)/shard_map/emit/pallas_call | solution.py:495

commit v3 on v2

v3 whole, which is shorter than its diff:
```python
import functools

import jax
import jax.numpy as jnp
from jax import lax
from jax.experimental import pallas as pl
from jax.experimental.pallas import tpu as pltpu
from jax.sharding import PartitionSpec as P

HD = 128
MESH = pl.DeviceIdType.MESH
VM = pl.BlockSpec(memory_space=pltpu.VMEM)
ANY = pl.BlockSpec(memory_space=pl.ANY)


def remote(src, dst, send, recv, device):
    return pltpu.make_async_remote_copy(
        src_ref=src, dst_ref=dst, send_sem=send, recv_sem=recv, device_id=device, device_id_type=MESH
    )


def each(lo, hi, act):
    def body(i, carry):
        act(i)
        return carry

    lax.fori_loop(lo, hi, body, 0)


def whole_kernel(
    n, tp, heads, rows, block, per,
    bytes_hbm, pob_hbm, first_hbm, moved_hbm, w_hbm, d_hbm,
    attn_ref, grad_ref,
    bytes_ref, pob_ref, first_ref, moved_ref, wbuf, d_ref,
    blk, came, pooled, own3, qb, gb, kb, vb, pa, ob, dqb, dkv, xkv, dka, dva,
    o_in, dq_in, dkv_in, part, own_part, lo_part, hi_part, tally,
    in_sem, w_sem, send_nb, recv_nb, send_x, recv_x, send_f, recv_f, send_m, recv_m,
    send_h, recv_o, recv_b, send_r, recv_r,
):
    pairs = n // 2
    groups = pairs // heads
    stride = 2 * groups
    total = n * rows
    half = rows // 2
    scale = HD ** (-0.5)
    bf, f32 = jnp.bfloat16, jnp.float32
    me, mt = lax.axis_index("ctx"), lax.axis_index("tp")
    sub = lax.rem(mt, 2)
    base = mt - sub
    mate = (me, base + 1 - sub)
    parity, place = lax.rem(me, 2), me // 2
    source_tp = base + parity
    at_home = parity == sub
    my_head, my_group = place // groups, lax.rem(place, groups)
    offset = 2 * my_group + sub
    slot = me // stride
    left, right = lax.rem(me + n - 1, n), lax.rem(me + 1, n)
    has_left, has_right = me > 0, me < n - 1
    width = part.shape[2]

    def cols(head, count=1):
        return pl.ds(pl.multiple_of(head * HD, HD), count * HD)

    chunks = heads // per

    def order(s):
        if chunks % 2:
            return lax.rem(my_head // per + (chunks + 1) // 2 + s, chunks)
        here, mid = my_head // per, chunks // 2
        upper = here // mid
        if s < mid:
            return (1 - upper) * (chunks - 1 - s) + upper * s
        back = chunks - 1 - s
        return upper * mid + lax.rem(here + back, mid)

    barrier = pltpu.get_barrier_semaphore()

    def greet(i):
        peer = lax.rem(me + i, n)
        for core in range(2):
            pl.semaphore_signal(barrier, inc=1, device_id=(peer, base + core), device_id_type=MESH)

    pl.semaphore_signal(barrier, inc=1, device_id=mate, device_id_type=MESH)
    each(1, n, greet)
    for c in (me, left, right):
        for i in range(2, tp):
            pl.semaphore_signal(
                barrier, inc=1, device_id=(c, lax.rem(base + i, tp)), device_id_type=MESH
            )
    inputs = [
        pltpu.make_async_copy(src, dst, in_sem.at[i])
        for i, (src, dst) in enumerate((
            (pob_hbm, pob_ref), (first_hbm, first_ref), (moved_hbm, moved_ref), (bytes_hbm, bytes_ref),
            (d_hbm, d_ref),
        ))
    ]
    for copy in inputs:
        copy.start()
    loads = [pltpu.make_async_copy(w_hbm.at[j], wbuf.at[j], w_sem.at[j]) for j in range(3)]
    for copy in inputs[:3]:
        copy.wait()

    def plan(c):
        below = moved_ref[1, lax.rem(c + n - 1, n)]
        above = moved_ref[0, lax.rem(c + 1, n)]
        start = first_ref[c]
        end = jnp.where(c == n - 1, total, first_ref[lax.rem(c + 1, n)])
        return start, end, below, above, moved_ref[0, c], moved_ref[1, c]

    def numbers(c, rank):
        start, end, below, above, low, high = plan(c)
        return jnp.where(
            rank < below,
            start - below + rank,
            jnp.where(rank >= rows - above, end + rank - (rows - above), start + low + rank - below),
        )

    start, end, below, above, low, high = plan(me)
    count = end - start
    rank = lax.broadcasted_iota(jnp.int32, (2 * rows, 1), 0)
    own_rank = rank - 2 * half
    own_local = jnp.where((own_rank >= below) & (own_rank < rows - above), low + own_rank - below, -1)
    up = jnp.where(rank - half < high, count - high + rank - half, -1)
    wanted = jnp.where(rank < half, rank - half + low, jnp.where(rank < 2 * half, up, own_local))
    pob = pob_ref[...]
    member = (pob == wanted).astype(f32)
    lengths = jnp.maximum(jnp.sum(member, axis=1, keepdims=True), 1.0)
    inputs[3].wait()
    for j in (1, 0, 2):
        loads[j].start()
    means = (
        jnp.dot(member.astype(bf), bytes_ref[...], preferred_element_type=f32) / lengths
    ).astype(bf)
    blk[0] = means[:half]
    blk[1] = means[half : 2 * half]

    @pl.when(me == 0)
    def _():
        came[1] = jnp.zeros_like(came[1])
        lo_part[...] = jnp.zeros_like(lo_part)

    @pl.when(me == n - 1)
    def _():
        came[0] = jnp.zeros_like(came[0])
        hi_part[...] = jnp.zeros_like(hi_part)

    pl.semaphore_wait(barrier, 2 * n - 1 + 3 * (tp - 2))
    to_left = remote(blk.at[0], came.at[0], send_nb.at[0], recv_nb.at[0], (left, mt))
    to_right = remote(blk.at[1], came.at[1], send_nb.at[1], recv_nb.at[1], (right, mt))
    pl.when(has_left)(to_left.start)
    pl.when(has_right)(to_right.start)

    def amount(count):
        return tally.at[pl.ds(0, count)]

    def came_in(sem, count):
        remote(amount(count), amount(count), sem, sem, mate).wait_recv()

    def went_out(sem, count):
        remote(amount(count), amount(count), sem, sem, mate).wait_send()

    def but_own(wait, sem, count, own=1):
        pl.when(at_home)(lambda: wait(sem, count - own))
        pl.when(jnp.logical_not(at_home))(lambda: wait(sem, count))

    def start_each(lo, hi, make):
        def act(i):
            other, copy = make(i)
            pl.when(other != me)(copy.start)

        each(lo, hi, act)

    def send_block(a, ref, out):
        def make(i):
            chip = 2 * i + sub
            return chip, remote(
                ref.at[:, cols(i // groups)], out.at[place, parity], send_x.at[a], recv_x.at[a],
                (chip, base + parity),
            )

        return make

    def send_query(a, ref, out):
        def make(h):
            chip = 2 * (h * groups + my_group) + sub
            return chip, remote(
                ref.at[:, cols(h)], out.at[slot], send_x.at[a], recv_x.at[a], (chip, base + parity)
            )

        return make

    def forward(a, ref):
        return remote(ref.at[:, sub], ref.at[:, sub], send_f.at[a], recv_f.at[a], mate)

    def back_query(a, ref, out):
        def make(j):
            c = j * stride + offset
            return c, remote(
                ref.at[j], out.at[:, cols(my_head)], send_h.at[a], recv_o.at[0] if a == 0 else recv_b.at[my_head // per],
                (c, source_tp),
            )

        return make

    def back_block(a):
        def make(i):
            c = 2 * i + sub
            return c, remote(
                dkv.at[a, i, sub], dkv_in.at[a, my_group, :, cols(my_head)], send_h.at[2 + a],
                recv_b.at[my_head // per], (c, source_tp),
            )

        return make

    send_g, send_q = send_query(3, d_ref, gb), send_query(2, own3.at[0], qb)
    send_k, send_v = send_block(0, own3.at[1], kb), send_block(1, own3.at[2], vb)
    lane = lax.broadcasted_iota(jnp.int32, (1, total), 1)

    def number_keys(c, ids):
        return jnp.where((lane >= c * rows) & (lane < (c + 1) * rows), numbers(c, lane - c * rows), ids)

    kid = lax.fori_loop(0, n, number_keys, jnp.zeros((1, total), jnp.int32))
    dka[...] = jnp.zeros_like(dka)
    dva[...] = jnp.zeros_like(dva)
    pl.when(has_left)(to_right.wait_recv)
    pl.when(has_right)(to_left.wait_recv)
    pooled[pl.ds(0, half)] = means[2 * half : 3 * half] + came[1]
    pooled[pl.ds(half, half)] = means[3 * half :] + came[0]
    mine = cols(my_head)
    for j, make in ((1, send_k), (0, send_q), (2, send_v)):
        loads[j].wait()
        for s in range(chunks):
            chunk = order(s)
            span = cols(chunk * per, per)
            own3[j, :, span] = jnp.dot(
                pooled[...], wbuf[j, :, span], preferred_element_type=f32
            ).astype(bf)
            each_head = per if j == 0 else per * groups
            start_each(chunk * each_head, (chunk + 1) * each_head, make)
    inputs[4].wait()
    start_each(0, heads, send_g)

    @pl.when(parity == sub)
    def _():
        qb[slot] = own3[0, :, mine]
        kb[place, parity] = own3[1, :, mine]
        vb[place, parity] = own3[2, :, mine]
        gb[slot] = d_ref[:, mine]

    over_last = (((1,), (1,)), ((), ()))
    over_first = (((0,), (0,)), ((), ()))
    back_o, back_q = back_query(0, ob, o_in), back_query(1, dqb, dq_in)
    back_k, back_v = back_block(0), back_block(1)
    row = lax.broadcasted_iota(jnp.int32, (rows, 1), 0)
    step_keys = max(2, 128 // rows)

    def reach_of(b):
        if b < 0:
            return 0
        reach = min(n, (b + 1) * block * stride + 1)
        return min(n, -(-reach // step_keys) * step_keys)

    def at(c):
        return pl.ds(pl.multiple_of(c * rows, rows), rows)

    def settled_sum(a, c):
        return dka[at(c)] * scale if a == 0 else dva[at(c)]

    def hand_over(step, lo, hi):
        def act(i):
            for a in range(2):
                dkv[a, i, 1 - sub] = settled_sum(a, 2 * i + 1 - sub).astype(bf)

        each(lo // 2, hi // 2, act)
        span = pl.ds(lo // 2, (hi - lo) // 2)
        remote(dkv.at[:, span, 1 - sub], xkv.at[:, span], send_m.at[step], recv_m.at[step], mate).start()

    def send_home(step, lo, hi):
        came_in(recv_m.at[step], hi - lo)

        def act(i):
            for a, make in enumerate((back_k, back_v)):
                dkv[a, i, sub] = (settled_sum(a, 2 * i + sub) + xkv[a, i].astype(f32)).astype(bf)
                other, copy = make(i)
                pl.when(other != me)(copy.start)

        each(lo // 2, hi // 2, act)

    steps = list(reversed(range(heads // block)))
    but_own(came_in, recv_x.at[0], pairs)
    forward(0, kb).start()
    but_own(came_in, recv_x.at[2], heads)
    came_in(recv_f.at[0], pairs)
    for b in steps:
        lo, reach = b * block, reach_of(b)
        keys = reach * rows
        q = qb[pl.ds(lo, block)].reshape(block * rows, HD)
        k = kb[pl.ds(0, reach // 2)].reshape(keys, HD)
        qid = jnp.concatenate([numbers((lo + j) * stride + offset, row) for j in range(block)], axis=0)
        allowed = qid >= kid[:, :keys]
        score = lax.dot_general(q, k, over_last, preferred_element_type=f32) * scale
        score = jnp.where(allowed, score, -jnp.inf)
        top = jnp.max(score, axis=1, keepdims=True)
        e = jnp.exp(score - top)
        pa[b, :, pl.ds(0, keys)] = e * (1.0 / jnp.sum(e, axis=1, keepdims=True))
    but_own(came_in, recv_x.at[1], pairs)
    forward(1, vb).start()
    came_in(recv_f.at[1], pairs)
    for b in steps:
        lo, reach = b * block, reach_of(b)
        keys = reach * rows
        v = vb[pl.ds(0, reach // 2)].reshape(keys, HD)
        out = jnp.dot(pa[b, :, pl.ds(0, keys)].astype(bf), v, preferred_element_type=f32).astype(bf)
        ob[pl.ds(lo, block)] = out.reshape(block, rows, HD)
        start_each(lo, lo + block, back_o)
    but_own(came_in, recv_x.at[3], heads)
    late = None
    for b in steps:
        lo = b * block
        reach, settled = reach_of(b), reach_of(b - 1)
        keys = reach * rows
        q = qb[pl.ds(lo, block)].reshape(block * rows, HD)
        g = gb[pl.ds(lo, block)].reshape(block * rows, HD)
        k = kb[pl.ds(0, reach // 2)].reshape(keys, HD)
        v = vb[pl.ds(0, reach // 2)].reshape(keys, HD)
        out = ob[pl.ds(lo, block)].reshape(block * rows, HD)
        prob = pa[b, :, pl.ds(0, keys)]
        delta = jnp.sum(g.astype(f32) * out.astype(f32), axis=1, keepdims=True)
        dprob = lax.dot_general(g, v, over_last, preferred_element_type=f32)
        dscore = (prob * (dprob - delta)).astype(bf)
        dq = (jnp.dot(dscore, k, preferred_element_type=f32) * scale).astype(bf)
        dqb[pl.ds(lo, block)] = dq.reshape(block, rows, HD)
        dka[pl.ds(0, keys)] += lax.dot_general(dscore, q, over_first, preferred_element_type=f32)
        dva[pl.ds(0, keys)] += lax.dot_general(prob.astype(bf), g, over_first, preferred_element_type=f32)
        start_each(lo, lo + block, back_q)
        if reach > settled:
            hand_over(b, settled, reach)
        if late is not None:
            send_home(*late)
        late = (b, settled, reach) if reach > settled else None
    if late is not None:
        send_home(*late)

    @pl.when(parity == sub)
    def _():
        o_in[:, mine] = ob[slot]
        dq_in[:, mine] = dqb[slot]
        for a in range(2):
            dkv_in[a, my_group, :, mine] = dkv[a, place, parity]

    but_own(came_in, recv_o.at[0], heads)
    attn_ref[...] = o_in[...]
    partial = jnp.zeros((rows, pooled.shape[1]), f32)
    for s in reversed(range(chunks)):
        chunk = order(s)
        span = cols(chunk * per, per)
        blocks = per + 2 * per * groups
        own_chunk = at_home & (chunk == my_head // per)
        pl.when(own_chunk)(lambda: came_in(recv_b.at[chunk], blocks - 3))
        pl.when(jnp.logical_not(own_chunk))(lambda: came_in(recv_b.at[chunk], blocks))
        for j in range(3):
            if j == 0:
                summed = dq_in[:, span]
            elif groups == 1:
                summed = dkv_in[j - 1, 0, :, span]
            else:
                summed = dkv_in[j - 1, 0, :, span].astype(f32)
                for i in range(1, groups):
                    summed = summed + dkv_in[j - 1, i, :, span].astype(f32)
                summed = summed.astype(bf)
            partial += lax.dot_general(summed, wbuf[j, :, span], over_last, preferred_element_type=f32)
    for t in range(tp):
        part[t] = partial[:, t * width : (t + 1) * width].astype(bf)
    edge_lo, edge_hi = pl.ds(0, half), pl.ds(rows - half, half)
    def give_back(a, piece, into, peer):
        return [
            remote(piece(t), into.at[mt], send_r.at[a], recv_r.at[a], (peer, t))
            for t in (lax.rem(mt + i, tp) for i in range(1 if a == 2 else 0, tp))
        ]

    @pl.when(has_left)
    def _():
        for copy in give_back(0, lambda t: part.at[t, edge_lo], hi_part, left):
            copy.start()

    @pl.when(has_right)
    def _():
        for copy in give_back(1, lambda t: part.at[t, edge_hi], lo_part, right):
            copy.start()

    for copy in give_back(2, lambda t: part.at[t], own_part, me):
        copy.start()
    own_part[mt] = part[mt]
    target = jnp.where(
        pob < low,
        half - low + pob,
        jnp.where(pob >= count - high, half + rows + pob - (count - high), half + below + pob - low),
    )
    chooser = (target == lax.broadcasted_iota(jnp.int32, (2 * rows, 1), 0)).astype(f32)
    sizes = jnp.maximum(jnp.sum(chooser, axis=1, keepdims=True), 1.0)
    pl.when(has_left)(to_left.wait_send)
    pl.when(has_right)(to_right.wait_send)
    for a in range(2):
        but_own(went_out, send_x.at[a], pairs)
        but_own(went_out, send_x.at[2 + a], heads)
        but_own(went_out, send_h.at[a], heads)
        but_own(went_out, send_h.at[2 + a], pairs)
        went_out(send_f.at[a], pairs)
    for b in steps:
        if reach_of(b) > reach_of(b - 1):
            went_out(send_m.at[b], reach_of(b) - reach_of(b - 1))
    others = own_part.at[pl.ds(0, tp - 1)]
    for here, a, ref in ((has_right, 0, hi_part), (has_left, 1, lo_part)):
        pl.when(here)(lambda: remote(ref, ref, send_r.at[a], recv_r.at[a], mate).wait_recv())
    remote(others, others, send_r.at[2], recv_r.at[2], mate).wait_recv()
    for here, a, ref in ((has_left, 0, hi_part), (has_right, 1, lo_part)):
        pl.when(here)(lambda: remote(ref, ref, send_r.at[a], recv_r.at[a], mate).wait_send())
    remote(others, others, send_r.at[2], recv_r.at[2], mate).wait_send()

    def over_tp(ref):
        value = ref[0].astype(f32)
        for i in range(1, tp):
            value = value + ref[i].astype(f32)
        return value

    returned = jnp.concatenate([over_tp(lo_part), over_tp(own_part), over_tp(hi_part)], axis=0)
    shares = (returned.astype(bf).astype(f32) / sizes).astype(bf)
    grad_ref[...] = lax.dot_general(
        chooser.astype(bf), shares, over_first, preferred_element_type=f32
    ).astype(bf)


def emit_kernel(a_ref, g_ref, a_out, g_out, sem):
    copies = [
        pltpu.make_async_copy(src, dst, sem.at[i]) for i, (src, dst) in enumerate(((a_ref, a_out), (g_ref, g_out)))
    ]
    for copy in copies:
        copy.start()
    for copy in copies:
        copy.wait()


def shards(byte_states, patch_of_byte, patch_first, moved, w_qkv, d_attn):
    n, tp = lax.axis_size("ctx"), lax.axis_size("tp")
    rows, feats = d_attn.shape
    size, model = byte_states.shape
    heads = feats // HD
    pairs = n // 2
    groups = pairs // heads
    total = n * rows
    half = rows // 2
    width = model // tp
    block = per = 2 if heads % 2 == 0 else 1
    steps = heads // block
    assert tp % 2 == 0 and n % 2 == 0 and pairs % heads == 0
    bf, f32, i32 = jnp.bfloat16, jnp.float32, jnp.int32
    dma = pltpu.SemaphoreType.DMA
    results = pl.pallas_call(
        functools.partial(whole_kernel, n, tp, heads, rows, block, per),
        out_shape=[pltpu.VMEM((rows, feats), bf), pltpu.VMEM((size, width), bf)],
        in_specs=[ANY] * 6,
        out_specs=[VM] * 2,
        scratch_shapes=[
            pltpu.VMEM((size, model), bf), pltpu.VMEM((1, size), i32),
            pltpu.SMEM((n,), i32), pltpu.SMEM((2, n), i32),
            pltpu.VMEM(w_qkv.shape, bf), pltpu.VMEM((rows, feats), bf),
            pltpu.VMEM((2, half, model), bf), pltpu.VMEM((2, half, model), bf),
            pltpu.VMEM((rows, model), bf), pltpu.VMEM((3, rows, feats), bf),
            pltpu.VMEM((heads, rows, HD), bf), pltpu.VMEM((heads, rows, HD), bf),
            pltpu.VMEM((pairs, 2, rows, HD), bf), pltpu.VMEM((pairs, 2, rows, HD), bf),
            pltpu.VMEM((steps, block * rows, total), f32),
            pltpu.VMEM((heads, rows, HD), bf), pltpu.VMEM((heads, rows, HD), bf),
            pltpu.VMEM((2, pairs, 2, rows, HD), bf), pltpu.VMEM((2, pairs, rows, HD), bf),
            pltpu.VMEM((total, HD), f32), pltpu.VMEM((total, HD), f32),
            pltpu.VMEM((rows, feats), bf), pltpu.VMEM((rows, feats), bf),
            pltpu.VMEM((2, groups, rows, feats), bf),
            pltpu.VMEM((tp, rows, width), bf), pltpu.VMEM((tp, rows, width), bf),
            pltpu.VMEM((tp, half, width), bf), pltpu.VMEM((tp, half, width), bf),
            pltpu.VMEM((max(n, per + 2 * per * groups), rows, HD), bf),
            dma((5,)), dma((3,)), dma((2,)), dma((2,)), dma((4,)), dma((4,)), dma((2,)), dma((2,)),
            dma((steps,)), dma((steps,)), dma((4,)), dma((1,)), dma((heads // per,)), dma((3,)), dma((3,)),
        ],
        compiler_params=pltpu.CompilerParams(
            collective_id=0, has_side_effects=True, vmem_limit_bytes=60 << 20
        ),
        name="whole",
    )(byte_states, patch_of_byte.reshape(1, size), patch_first, moved, w_qkv, d_attn)
    results = [pltpu.with_memory_space_constraint(x, pltpu.VMEM) for x in results]
    return tuple(pl.pallas_call(
        emit_kernel,
        out_shape=[jax.ShapeDtypeStruct((rows, feats), bf), jax.ShapeDtypeStruct((size, width), bf)],
        in_specs=[VM, VM],
        out_specs=[ANY] * 2,
        scratch_shapes=[dma((2,))],
        name="emit",
    )(*results))


def solution(mesh):
    placed = (P("ctx", None), P("ctx"), P(), P(), P(None, None, "tp"), P("ctx", "tp"))
    return jax.shard_map(
        shards,
        mesh=mesh,
        in_specs=placed,
        out_specs=(P("ctx", "tp"), P("ctx", "tp")),
        check_vma=False,
    )
```

time: 50.4 us -> 45.1 us (0.89)
  Pallas kernels: 49.6 us -> 44.3 us
    pallas_call x1, Pallas kernels: 48.8 us -> 43.5 us  [shards(): pl.pallas_call(functools.partial(whole_kernel, n, tp, heads, rows, block,...]
where the time goes in v3:
time: 45.1 us; the launch traced here: 44.9 us
  Pallas kernels  44.3 us (98%)
  between operations  0.64 us (1%)
    pallas_call x1, Pallas kernels, shards(): pl.pallas_call(functools.partial(whole_kernel, n, tp, heads, rows, block,...  43.5 us

profile of v3, /device:TPU:0, one launch (start us, length us, event | category | flops | bytes accessed | tf_op | source)
XLA Modules:
  0.0 44.9 jit_solution(8754094201754394587)
XLA Ops:
  0.6 43.5 %whole.1 = (bf16[64,1024]{1,0:T(8,128)(2,1)S(1)}, bf16[256,512]{1,0:T(8,128)(2,1)S(1)}) custom-call(bf16[256,1024]{1,0:T(8,128)(2,1)} %bytes_hbm.1, s32[1,256]{1,0:T(1,128)} %bitcast.1, s32[16]{0:T(128)} %first_hbm.1, s32[2,16]{1,0:T(2,128)} %moved_hbm.1, bf16[3,1024,1024]{2,1,0:T(8,128)(2,1)} %w_hbm.1, bf16[64,1024]{1,0:T(8,128)(2,1)} %d_hbm.1), custom_call_target="tpu_custom_call" | custom-call | tf_op jit(solution)/shard_map/whole/pallas_call | solution.py:458
  44.2 0.8 %emit.1 = (bf16[64,1024]{1,0:T(8,128)(2,1)}, bf16[256,512]{1,0:T(8,128)(2,1)}) custom-call(bf16[64,1024]{1,0:T(8,128)(2,1)S(1)} %get-tuple-element.4.a_ref, bf16[256,512]{1,0:T(8,128)(2,1)S(1)} %get-tuple-element.5.g_ref), custom_call_target="tpu_custom_call" | custom-call | tf_op jit(solution)/shard_map/emit/pallas_call | solution.py:489

commit v4 on v3

--- a/solution.py
+++ b/solution.py
@@ -126,7 +126,7 @@
     member = (pob == wanted).astype(f32)
     lengths = jnp.maximum(jnp.sum(member, axis=1, keepdims=True), 1.0)
     inputs[3].wait()
-    for j in (1, 0, 2):
+    for j in (1, 2, 0):
         loads[j].start()
     means = (
         jnp.dot(member.astype(bf), bytes_ref[...], preferred_element_type=f32) / lengths
@@ -196,8 +196,7 @@
         def make(j):
             c = j * stride + offset
             return c, remote(
-                ref.at[j], out.at[:, cols(my_head)], send_h.at[a], recv_o.at[0] if a == 0 else recv_b.at[my_head // per],
-                (c, source_tp),
+                ref.at[j], out.at[:, cols(my_head)], send_h.at[a], recv_o.at[a], (c, source_tp)
             )
 
         return make
@@ -214,6 +213,10 @@
 
     send_g, send_q = send_query(3, d_ref, gb), send_query(2, own3.at[0], qb)
     send_k, send_v = send_block(0, own3.at[1], kb), send_block(1, own3.at[2], vb)
+    inputs[4].wait()
+    early = chunks // 2
+    for s in range(early):
+        start_each(order(s) * per, order(s) * per + per, send_g)
     lane = lax.broadcasted_iota(jnp.int32, (1, total), 1)
 
     def number_keys(c, ids):
@@ -227,7 +230,7 @@
     pooled[pl.ds(0, half)] = means[2 * half : 3 * half] + came[1]
     pooled[pl.ds(half, half)] = means[3 * half :] + came[0]
     mine = cols(my_head)
-    for j, make in ((1, send_k), (0, send_q), (2, send_v)):
+    for j, make in ((1, send_k), (2, send_v), (0, send_q)):
         loads[j].wait()
         for s in range(chunks):
             chunk = order(s)
@@ -237,8 +240,8 @@
             ).astype(bf)
             each_head = per if j == 0 else per * groups
             start_each(chunk * each_head, (chunk + 1) * each_head, make)
-    inputs[4].wait()
-    start_each(0, heads, send_g)
+    for s in range(early, chunks):
+        start_each(order(s) * per, order(s) * per + per, send_g)
 
     @pl.when(parity == sub)
     def _():
@@ -289,40 +292,37 @@
     steps = list(reversed(range(heads // block)))
     but_own(came_in, recv_x.at[0], pairs)
     forward(0, kb).start()
+    but_own(came_in, recv_x.at[1], pairs)
+    forward(1, vb).start()
     but_own(came_in, recv_x.at[2], heads)
     came_in(recv_f.at[0], pairs)
-    for b in steps:
+    came_in(recv_f.at[1], pairs)
+
+    def attend(b):
         lo, reach = b * block, reach_of(b)
         keys = reach * rows
         q = qb[pl.ds(lo, block)].reshape(block * rows, HD)
         k = kb[pl.ds(0, reach // 2)].reshape(keys, HD)
+        v = vb[pl.ds(0, reach // 2)].reshape(keys, HD)
         qid = jnp.concatenate([numbers((lo + j) * stride + offset, row) for j in range(block)], axis=0)
         allowed = qid >= kid[:, :keys]
         score = lax.dot_general(q, k, over_last, preferred_element_type=f32) * scale
         score = jnp.where(allowed, score, -jnp.inf)
         top = jnp.max(score, axis=1, keepdims=True)
         e = jnp.exp(score - top)
-        pa[b, :, pl.ds(0, keys)] = e * (1.0 / jnp.sum(e, axis=1, keepdims=True))
-    but_own(came_in, recv_x.at[1], pairs)
-    forward(1, vb).start()
-    came_in(recv_f.at[1], pairs)
-    for b in steps:
-        lo, reach = b * block, reach_of(b)
-        keys = reach * rows
-        v = vb[pl.ds(0, reach // 2)].reshape(keys, HD)
-        out = jnp.dot(pa[b, :, pl.ds(0, keys)].astype(bf), v, preferred_element_type=f32).astype(bf)
+        prob = e * (1.0 / jnp.sum(e, axis=1, keepdims=True))
+        pa[b, :, pl.ds(0, keys)] = prob
+        out = jnp.dot(prob.astype(bf), v, preferred_element_type=f32).astype(bf)
         ob[pl.ds(lo, block)] = out.reshape(block, rows, HD)
         start_each(lo, lo + block, back_o)
-    but_own(came_in, recv_x.at[3], heads)
-    late = None
-    for b in steps:
+
+    def differentiate(b):
         lo = b * block
-        reach, settled = reach_of(b), reach_of(b - 1)
-        keys = reach * rows
+        keys = reach_of(b) * rows
         q = qb[pl.ds(lo, block)].reshape(block * rows, HD)
         g = gb[pl.ds(lo, block)].reshape(block * rows, HD)
-        k = kb[pl.ds(0, reach // 2)].reshape(keys, HD)
-        v = vb[pl.ds(0, reach // 2)].reshape(keys, HD)
+        k = kb[pl.ds(0, reach_of(b) // 2)].reshape(keys, HD)
+        v = vb[pl.ds(0, reach_of(b) // 2)].reshape(keys, HD)
         out = ob[pl.ds(lo, block)].reshape(block * rows, HD)
         prob = pa[b, :, pl.ds(0, keys)]
         delta = jnp.sum(g.astype(f32) * out.astype(f32), axis=1, keepdims=True)
@@ -330,16 +330,34 @@
         dscore = (prob * (dprob - delta)).astype(bf)
         dq = (jnp.dot(dscore, k, preferred_element_type=f32) * scale).astype(bf)
         dqb[pl.ds(lo, block)] = dq.reshape(block, rows, HD)
+        start_each(lo, lo + block, back_q)
         dka[pl.ds(0, keys)] += lax.dot_general(dscore, q, over_first, preferred_element_type=f32)
         dva[pl.ds(0, keys)] += lax.dot_general(prob.astype(bf), g, over_first, preferred_element_type=f32)
-        start_each(lo, lo + block, back_q)
-        if reach > settled:
-            hand_over(b, settled, reach)
-        if late is not None:
-            send_home(*late)
-        late = (b, settled, reach) if reach > settled else None
-    if late is not None:
-        send_home(*late)
+
+    middle = n // 2 // step_keys * step_keys
+    whole = [(i, lo, hi) for i, (lo, hi) in enumerate(((0, middle), (middle, n))) if hi > lo]
+    falling = (steps, {b: [(b, reach_of(b - 1), reach_of(b))] for b in steps if reach_of(b) > reach_of(b - 1)})
+    rising = (steps[::-1], {steps[0]: whole})
+    upper = me >= n // 2
+    halves = [(upper, rising), (jnp.logical_not(upper), falling)] if len(steps) > 1 else [(me >= 0, falling)]
+
+    def work(blocks, spans):
+        for b in blocks:
+            attend(b)
+        but_own(came_in, recv_x.at[3], heads)
+        late = []
+        for b in blocks:
+            differentiate(b)
+            for span in spans.get(b, ()):
+                hand_over(*span)
+            for span in late:
+                send_home(*span)
+            late = spans.get(b, [])
+        for span in late:
+            send_home(*span)
+
+    for here, plan_of in halves:
+        pl.when(here)(functools.partial(work, *plan_of))
 
     @pl.when(parity == sub)
     def _():
@@ -350,18 +368,17 @@
 
     but_own(came_in, recv_o.at[0], heads)
     attn_ref[...] = o_in[...]
-    partial = jnp.zeros((rows, pooled.shape[1]), f32)
+    but_own(came_in, recv_o.at[1], heads)
+    partial = lax.dot_general(dq_in[...], wbuf[0], over_last, preferred_element_type=f32)
     for s in reversed(range(chunks)):
         chunk = order(s)
         span = cols(chunk * per, per)
-        blocks = per + 2 * per * groups
+        blocks = 2 * per * groups
         own_chunk = at_home & (chunk == my_head // per)
-        pl.when(own_chunk)(lambda: came_in(recv_b.at[chunk], blocks - 3))
+        pl.when(own_chunk)(lambda: came_in(recv_b.at[chunk], blocks - 2))
         pl.when(jnp.logical_not(own_chunk))(lambda: came_in(recv_b.at[chunk], blocks))
-        for j in range(3):
-            if j == 0:
-                summed = dq_in[:, span]
-            elif groups == 1:
+        for j in (1, 2):
+            if groups == 1:
                 summed = dkv_in[j - 1, 0, :, span]
             else:
                 summed = dkv_in[j - 1, 0, :, span].astype(f32)
@@ -406,9 +423,14 @@
         but_own(went_out, send_h.at[a], heads)
         but_own(went_out, send_h.at[2 + a], pairs)
         went_out(send_f.at[a], pairs)
-    for b in steps:
-        if reach_of(b) > reach_of(b - 1):
-            went_out(send_m.at[b], reach_of(b) - reach_of(b - 1))
+
+    def handed_over(blocks, spans):
+        for b in blocks:
+            for i, lo, hi in spans.get(b, ()):
+                went_out(send_m.at[i], hi - lo)
+
+    for here, plan_of in halves:
+        pl.when(here)(functools.partial(handed_over, *plan_of))
     others = own_part.at[pl.ds(0, tp - 1)]
     for here, a, ref in ((has_right, 0, hi_part), (has_left, 1, lo_part)):
         pl.when(here)(lambda: remote(ref, ref, send_r.at[a], recv_r.at[a], mate).wait_recv())
@@ -478,7 +500,7 @@
             pltpu.VMEM((tp, half, width), bf), pltpu.VMEM((tp, half, width), bf),
             pltpu.VMEM((max(n, per + 2 * per * groups), rows, HD), bf),
             dma((5,)), dma((3,)), dma((2,)), dma((2,)), dma((4,)), dma((4,)), dma((2,)), dma((2,)),
-            dma((steps,)), dma((steps,)), dma((4,)), dma((1,)), dma((heads // per,)), dma((3,)), dma((3,)),
+            dma((max(2, steps),)), dma((max(2, steps),)), dma((4,)), dma((2,)), dma((heads // per,)), dma((3,)), dma((3,)),
         ],
         compiler_params=pltpu.CompilerParams(
             collective_id=0, has_side_effects=True, vmem_limit_bytes=60 << 20

time: 45.1 us -> 41.9 us (0.929)
  Pallas kernels: 44.3 us -> 40.7 us
    pallas_call x1, Pallas kernels: 43.5 us -> 39.9 us  [shards(): pl.pallas_call(functools.partial(whole_kernel, n, tp, heads, rows, block,...]
where the time goes in v4:
time: 41.9 us; the launch traced here: 41.3 us
  Pallas kernels  40.7 us (97%)
  between operations  0.64 us (2%)
    pallas_call x1, Pallas kernels, shards(): pl.pallas_call(functools.partial(whole_kernel, n, tp, heads, rows, block,...  39.9 us

profile of v4, /device:TPU:0, one launch (start us, length us, event | category | flops | bytes accessed | tf_op | source)
XLA Modules:
  0.0 41.3 jit_solution(15948424726487970552)
XLA Ops:
  0.6 39.9 %whole.1 = (bf16[64,1024]{1,0:T(8,128)(2,1)S(1)}, bf16[256,512]{1,0:T(8,128)(2,1)S(1)}) custom-call(bf16[256,1024]{1,0:T(8,128)(2,1)} %bytes_hbm.1, s32[1,256]{1,0:T(1,128)} %bitcast.1, s32[16]{0:T(128)} %first_hbm.1, s32[2,16]{1,0:T(2,128)} %moved_hbm.1, bf16[3,1024,1024]{2,1,0:T(8,128)(2,1)} %w_hbm.1, bf16[64,1024]{1,0:T(8,128)(2,1)} %d_hbm.1), custom_call_target="tpu_custom_call" | custom-call | tf_op jit(solution)/shard_map/whole/pallas_call | solution.py:480
  40.5 0.8 %emit.1 = (bf16[64,1024]{1,0:T(8,128)(2,1)}, bf16[256,512]{1,0:T(8,128)(2,1)}) custom-call(bf16[64,1024]{1,0:T(8,128)(2,1)S(1)} %get-tuple-element.4.a_ref, bf16[256,512]{1,0:T(8,128)(2,1)S(1)} %get-tuple-element.5.g_ref), custom_call_target="tpu_custom_call" | custom-call | tf_op jit(solution)/shard_map/emit/pallas_call | solution.py:511

commit v5 on v4

--- a/solution.py
+++ b/solution.py
@@ -32,10 +32,10 @@
     bytes_hbm, pob_hbm, first_hbm, moved_hbm, w_hbm, d_hbm,
     attn_ref, grad_ref,
     bytes_ref, pob_ref, first_ref, moved_ref, wbuf, d_ref,
-    blk, came, pooled, own3, qb, gb, kb, vb, pa, ob, dqb, dkv, xkv, dka, dva,
+    blk, came, pooled, own3, qb, gb, kb, vb, pa, ob, dqb, dkv, xkv, dkva,
     o_in, dq_in, dkv_in, part, own_part, lo_part, hi_part, tally,
-    in_sem, w_sem, send_nb, recv_nb, send_x, recv_x, send_f, recv_f, send_m, recv_m,
-    send_h, recv_o, recv_b, send_r, recv_r,
+    in_sem, w_sem, send_nb, recv_nb, send_x, recv_x, recv_q, send_f, recv_f, send_m, recv_m,
+    send_h, recv_o, recv_b, send_r, recv_r, word,
 ):
     pairs = n // 2
     groups = pairs // heads
@@ -75,18 +75,36 @@
 
     barrier = pltpu.get_barrier_semaphore()
 
+    window = -(-n // 4)
+
     def greet(i):
-        peer = lax.rem(me + i, n)
-        for core in range(2):
-            pl.semaphore_signal(barrier, inc=1, device_id=(peer, base + core), device_id_type=MESH)
+        for there, peer in ((me >= i, me - i), (me + i < n, me + i)):
+            @pl.when(there)
+            def _():
+                for core in range(2):
+                    pl.semaphore_signal(barrier, inc=1, device_id=(peer, base + core), device_id_type=MESH)
 
     pl.semaphore_signal(barrier, inc=1, device_id=mate, device_id_type=MESH)
-    each(1, n, greet)
-    for c in (me, left, right):
+    each(1, window + 1, greet)
+    for there, c in ((me >= 0, me), (has_left, me - 1), (has_right, me + 1)):
         for i in range(2, tp):
-            pl.semaphore_signal(
-                barrier, inc=1, device_id=(c, lax.rem(base + i, tp)), device_id_type=MESH
-            )
+            pl.when(there)(functools.partial(
+                pl.semaphore_signal, barrier, inc=1, device_id=(c, lax.rem(base + i, tp)), device_id_type=MESH
+            ))
+    beside = has_left.astype(jnp.int32) + has_right.astype(jnp.int32)
+    expected = 1 + 2 * (jnp.minimum(me, window) + jnp.minimum(n - 1 - me, window)) + (tp - 2) * (1 + beside)
+
+    def spread(round_):
+        far = window << round_
+        for there, peer in ((me >= far, me - far), (me + far < n, me + far)):
+            pl.when(there)(functools.partial(
+                pl.semaphore_signal, word.at[round_], inc=1, device_id=(peer, mt), device_id_type=MESH
+            ))
+
+    def heard(round_):
+        far = window << round_
+        pl.semaphore_wait(word.at[round_], (me >= far).astype(jnp.int32) + (me + far < n).astype(jnp.int32))
+
     inputs = [
         pltpu.make_async_copy(src, dst, in_sem.at[i])
         for i, (src, dst) in enumerate((
@@ -144,11 +162,14 @@
         came[0] = jnp.zeros_like(came[0])
         hi_part[...] = jnp.zeros_like(hi_part)
 
-    pl.semaphore_wait(barrier, 2 * n - 1 + 3 * (tp - 2))
+    pl.semaphore_wait(barrier, expected)
     to_left = remote(blk.at[0], came.at[0], send_nb.at[0], recv_nb.at[0], (left, mt))
     to_right = remote(blk.at[1], came.at[1], send_nb.at[1], recv_nb.at[1], (right, mt))
     pl.when(has_left)(to_left.start)
     pl.when(has_right)(to_right.start)
+    spread(0)
+    heard(0)
+    spread(1)
 
     def amount(count):
         return tally.at[pl.ds(0, count)]
@@ -184,7 +205,8 @@
         def make(h):
             chip = 2 * (h * groups + my_group) + sub
             return chip, remote(
-                ref.at[:, cols(h)], out.at[slot], send_x.at[a], recv_x.at[a], (chip, base + parity)
+                ref.at[:, cols(h)], out.at[slot], send_x.at[a],
+                recv_q.at[slot // block] if a == 2 else recv_x.at[a], (chip, base + parity),
             )
 
         return make
@@ -201,18 +223,16 @@
 
         return make
 
-    def back_block(a):
-        def make(i):
-            c = 2 * i + sub
-            return c, remote(
-                dkv.at[a, i, sub], dkv_in.at[a, my_group, :, cols(my_head)], send_h.at[2 + a],
-                recv_b.at[my_head // per], (c, source_tp),
-            )
-
-        return make
+    def back_block(i):
+        c = 2 * i + sub
+        return c, remote(
+            dkv.at[:, i, sub], dkv_in.at[:, my_group, :, cols(my_head)], send_h.at[2],
+            recv_b.at[my_head // per], (c, source_tp),
+        )
 
     send_g, send_q = send_query(3, d_ref, gb), send_query(2, own3.at[0], qb)
     send_k, send_v = send_block(0, own3.at[1], kb), send_block(1, own3.at[2], vb)
+    heard(1)
     inputs[4].wait()
     early = chunks // 2
     for s in range(early):
@@ -223,23 +243,29 @@
         return jnp.where((lane >= c * rows) & (lane < (c + 1) * rows), numbers(c, lane - c * rows), ids)
 
     kid = lax.fori_loop(0, n, number_keys, jnp.zeros((1, total), jnp.int32))
-    dka[...] = jnp.zeros_like(dka)
-    dva[...] = jnp.zeros_like(dva)
     pl.when(has_left)(to_right.wait_recv)
     pl.when(has_right)(to_left.wait_recv)
     pooled[pl.ds(0, half)] = means[2 * half : 3 * half] + came[1]
     pooled[pl.ds(half, half)] = means[3 * half :] + came[0]
     mine = cols(my_head)
-    for j, make in ((1, send_k), (2, send_v), (0, send_q)):
-        loads[j].wait()
-        for s in range(chunks):
-            chunk = order(s)
-            span = cols(chunk * per, per)
-            own3[j, :, span] = jnp.dot(
-                pooled[...], wbuf[j, :, span], preferred_element_type=f32
-            ).astype(bf)
-            each_head = per if j == 0 else per * groups
-            start_each(chunk * each_head, (chunk + 1) * each_head, make)
+    makers = (send_q, send_k, send_v)
+
+    def project(kinds):
+        for j, places in kinds:
+            loads[j].wait()
+            for s in places:
+                span = cols(order(s) * per, per)
+                own3[j, :, span] = jnp.dot(
+                    pooled[...], wbuf[j, :, span], preferred_element_type=f32
+                ).astype(bf)
+                each_head = per if j == 0 else per * groups
+                start_each(order(s) * each_head, (order(s) + 1) * each_head, makers[j])
+
+    outer = (me < n // 4) | (me >= n - n // 4)
+    far_first = list(range(chunks))
+    project(((1, far_first), (2, far_first)))
+    pl.when(outer)(lambda: project(((0, far_first),)))
+    pl.when(jnp.logical_not(outer))(lambda: project(((0, far_first[::-1]),)))
     for s in range(early, chunks):
         start_each(order(s) * per, order(s) * per + per, send_g)
 
@@ -253,7 +279,6 @@
     over_last = (((1,), (1,)), ((), ()))
     over_first = (((0,), (0,)), ((), ()))
     back_o, back_q = back_query(0, ob, o_in), back_query(1, dqb, dq_in)
-    back_k, back_v = back_block(0), back_block(1)
     row = lax.broadcasted_iota(jnp.int32, (rows, 1), 0)
     step_keys = max(2, 128 // rows)
 
@@ -267,7 +292,8 @@
         return pl.ds(pl.multiple_of(c * rows, rows), rows)
 
     def settled_sum(a, c):
-        return dka[at(c)] * scale if a == 0 else dva[at(c)]
+        value = dkva[at(c), a * HD : (a + 1) * HD]
+        return value * scale if a == 0 else value
 
     def hand_over(step, lo, hi):
         def act(i):
@@ -282,10 +308,10 @@
         came_in(recv_m.at[step], hi - lo)
 
         def act(i):
-            for a, make in enumerate((back_k, back_v)):
+            for a in range(2):
                 dkv[a, i, sub] = (settled_sum(a, 2 * i + sub) + xkv[a, i].astype(f32)).astype(bf)
-                other, copy = make(i)
-                pl.when(other != me)(copy.start)
+            other, copy = back_block(i)
+            pl.when(other != me)(copy.start)
 
         each(lo // 2, hi // 2, act)
 
@@ -294,7 +320,6 @@
     forward(0, kb).start()
     but_own(came_in, recv_x.at[1], pairs)
     forward(1, vb).start()
-    but_own(came_in, recv_x.at[2], heads)
     came_in(recv_f.at[0], pairs)
     came_in(recv_f.at[1], pairs)
 
@@ -314,9 +339,8 @@
         pa[b, :, pl.ds(0, keys)] = prob
         out = jnp.dot(prob.astype(bf), v, preferred_element_type=f32).astype(bf)
         ob[pl.ds(lo, block)] = out.reshape(block, rows, HD)
-        start_each(lo, lo + block, back_o)
-
-    def differentiate(b):
+
+    def differentiate(b, filled):
         lo = b * block
         keys = reach_of(b) * rows
         q = qb[pl.ds(lo, block)].reshape(block * rows, HD)
@@ -330,9 +354,20 @@
         dscore = (prob * (dprob - delta)).astype(bf)
         dq = (jnp.dot(dscore, k, preferred_element_type=f32) * scale).astype(bf)
         dqb[pl.ds(lo, block)] = dq.reshape(block, rows, HD)
-        start_each(lo, lo + block, back_q)
-        dka[pl.ds(0, keys)] += lax.dot_general(dscore, q, over_first, preferred_element_type=f32)
-        dva[pl.ds(0, keys)] += lax.dot_general(prob.astype(bf), g, over_first, preferred_element_type=f32)
+        blank = jnp.zeros_like(q)
+        both = lax.dot_general(
+            jnp.concatenate([dscore, prob.astype(bf)], axis=0),
+            jnp.concatenate(
+                [jnp.concatenate([q, blank], axis=1), jnp.concatenate([blank, g], axis=1)], axis=0
+            ),
+            over_first, preferred_element_type=f32,
+        )
+        old = min(keys, filled)
+        if old:
+            dkva[pl.ds(0, old)] += both[:old]
+        if keys > old:
+            dkva[pl.ds(old, keys - old)] = both[old:]
+        return max(keys, filled)
 
     middle = n // 2 // step_keys * step_keys
     whole = [(i, lo, hi) for i, (lo, hi) in enumerate(((0, middle), (middle, n))) if hi > lo]
@@ -342,17 +377,29 @@
     halves = [(upper, rising), (jnp.logical_not(upper), falling)] if len(steps) > 1 else [(me >= 0, falling)]
 
     def work(blocks, spans):
-        for b in blocks:
-            attend(b)
+        lead, first = max(1, len(blocks) // 2), blocks[:1]
+        for part_of in (first, blocks[1:]):
+            for b in part_of:
+                mine_too = at_home & (slot // block == b)
+                pl.when(mine_too)(lambda: came_in(recv_q.at[b], block - 1))
+                pl.when(jnp.logical_not(mine_too))(lambda: came_in(recv_q.at[b], block))
+            for b in part_of:
+                attend(b)
+            for b in part_of:
+                start_each(b * block, (b + 1) * block, back_o)
         but_own(came_in, recv_x.at[3], heads)
-        late = []
-        for b in blocks:
-            differentiate(b)
-            for span in spans.get(b, ()):
+        late, filled = [], 0
+        for part_of in (blocks[:lead], blocks[lead:]):
+            for b in part_of:
+                filled = differentiate(b, filled)
+            for b in part_of:
+                start_each(b * block, (b + 1) * block, back_q)
+            ready = [span for b in part_of for span in spans.get(b, ())]
+            for span in ready:
                 hand_over(*span)
             for span in late:
                 send_home(*span)
-            late = spans.get(b, [])
+            late = ready
         for span in late:
             send_home(*span)
 
@@ -421,7 +468,6 @@
         but_own(went_out, send_x.at[a], pairs)
         but_own(went_out, send_x.at[2 + a], heads)
         but_own(went_out, send_h.at[a], heads)
-        but_own(went_out, send_h.at[2 + a], pairs)
         went_out(send_f.at[a], pairs)
 
     def handed_over(blocks, spans):
@@ -429,6 +475,7 @@
             for i, lo, hi in spans.get(b, ()):
                 went_out(send_m.at[i], hi - lo)
 
+    but_own(went_out, send_h.at[2], 2 * pairs, 2)
     for here, plan_of in halves:
         pl.when(here)(functools.partial(handed_over, *plan_of))
     others = own_part.at[pl.ds(0, tp - 1)]
@@ -493,14 +540,14 @@
             pltpu.VMEM((steps, block * rows, total), f32),
             pltpu.VMEM((heads, rows, HD), bf), pltpu.VMEM((heads, rows, HD), bf),
             pltpu.VMEM((2, pairs, 2, rows, HD), bf), pltpu.VMEM((2, pairs, rows, HD), bf),
-            pltpu.VMEM((total, HD), f32), pltpu.VMEM((total, HD), f32),
+            pltpu.VMEM((total, 2 * HD), f32),
             pltpu.VMEM((rows, feats), bf), pltpu.VMEM((rows, feats), bf),
             pltpu.VMEM((2, groups, rows, feats), bf),
             pltpu.VMEM((tp, rows, width), bf), pltpu.VMEM((tp, rows, width), bf),
             pltpu.VMEM((tp, half, width), bf), pltpu.VMEM((tp, half, width), bf),
             pltpu.VMEM((max(n, per + 2 * per * groups), rows, HD), bf),
-            dma((5,)), dma((3,)), dma((2,)), dma((2,)), dma((4,)), dma((4,)), dma((2,)), dma((2,)),
-            dma((max(2, steps),)), dma((max(2, steps),)), dma((4,)), dma((2,)), dma((heads // per,)), dma((3,)), dma((3,)),
+            dma((5,)), dma((3,)), dma((2,)), dma((2,)), dma((4,)), dma((4,)), dma((steps,)), dma((2,)), dma((2,)),
+            dma((max(2, steps),)), dma((max(2, steps),)), dma((4,)), dma((2,)), dma((heads // per,)), dma((3,)), dma((3,)), pltpu.SemaphoreType.REGULAR((2,)),
         ],
         compiler_params=pltpu.CompilerParams(
             collective_id=0, has_side_effects=True, vmem_limit_bytes=60 << 20

time: 41.9 us -> 40.6 us (0.969)
  Pallas kernels: 40.7 us -> 39.7 us
    pallas_call x1, Pallas kernels: 39.9 us -> 38.9 us  [shards(): pl.pallas_call(functools.partial(whole_kernel, n, tp, heads, rows, block,...]
where the time goes in v5:
time: 40.6 us; the launch traced here: 40.3 us
  Pallas kernels  39.7 us (98%)
  between operations  0.64 us (2%)
    pallas_call x1, Pallas kernels, shards(): pl.pallas_call(functools.partial(whole_kernel, n, tp, heads, rows, block,...  38.9 us

profile of v5, /device:TPU:0, one launch (start us, length us, event | category | flops | bytes accessed | tf_op | source)
XLA Modules:
  0.0 40.3 jit_solution(17875920702790055464)
XLA Ops:
  0.6 38.9 %whole.1 = (bf16[64,1024]{1,0:T(8,128)(2,1)S(1)}, bf16[256,512]{1,0:T(8,128)(2,1)S(1)}) custom-call(bf16[256,1024]{1,0:T(8,128)(2,1)} %bytes_hbm.1, s32[1,256]{1,0:T(1,128)} %bitcast.1, s32[16]{0:T(128)} %first_hbm.1, s32[2,16]{1,0:T(2,128)} %moved_hbm.1, bf16[3,1024,1024]{2,1,0:T(8,128)(2,1)} %w_hbm.1, bf16[64,1024]{1,0:T(8,128)(2,1)} %d_hbm.1), custom_call_target="tpu_custom_call" | custom-call | tf_op jit(solution)/shard_map/whole/pallas_call | solution.py:527
  39.6 0.8 %emit.1 = (bf16[64,1024]{1,0:T(8,128)(2,1)}, bf16[256,512]{1,0:T(8,128)(2,1)}) custom-call(bf16[64,1024]{1,0:T(8,128)(2,1)S(1)} %get-tuple-element.4.a_ref, bf16[256,512]{1,0:T(8,128)(2,1)S(1)} %get-tuple-element.5.g_ref), custom_call_target="tpu_custom_call" | custom-call | tf_op jit(solution)/shard_map/emit/pallas_call | solution.py:558

commit v6 on v5

--- a/solution.py
+++ b/solution.py
@@ -34,8 +34,7 @@
     bytes_ref, pob_ref, first_ref, moved_ref, wbuf, d_ref,
     blk, came, pooled, own3, qb, gb, kb, vb, pa, ob, dqb, dkv, xkv, dkva,
     o_in, dq_in, dkv_in, part, own_part, lo_part, hi_part, tally,
-    in_sem, w_sem, send_nb, recv_nb, send_x, recv_x, recv_q, send_f, recv_f, send_m, recv_m,
-    send_h, recv_o, recv_b, send_r, recv_r, word,
+    in_sem, w_sem, send_nb, recv_nb, sent, recv_x, recv_q, recv_f, recv_m, recv_o, recv_b, send_r, recv_r, word,
 ):
     pairs = n // 2
     groups = pairs // heads
@@ -73,6 +72,15 @@
         back = chunks - 1 - s
         return upper * mid + lax.rem(here + back, mid)
 
+    inputs = [
+        pltpu.make_async_copy(src, dst, in_sem.at[i])
+        for i, (src, dst) in enumerate((
+            (pob_hbm, pob_ref), (first_hbm, first_ref), (moved_hbm, moved_ref), (bytes_hbm, bytes_ref),
+            (d_hbm, d_ref),
+        ))
+    ]
+    for copy in inputs:
+        copy.start()
     barrier = pltpu.get_barrier_semaphore()
 
     window = -(-n // 4)
@@ -105,15 +113,6 @@
         far = window << round_
         pl.semaphore_wait(word.at[round_], (me >= far).astype(jnp.int32) + (me + far < n).astype(jnp.int32))
 
-    inputs = [
-        pltpu.make_async_copy(src, dst, in_sem.at[i])
-        for i, (src, dst) in enumerate((
-            (pob_hbm, pob_ref), (first_hbm, first_ref), (moved_hbm, moved_ref), (bytes_hbm, bytes_ref),
-            (d_hbm, d_ref),
-        ))
-    ]
-    for copy in inputs:
-        copy.start()
     loads = [pltpu.make_async_copy(w_hbm.at[j], wbuf.at[j], w_sem.at[j]) for j in range(3)]
     for copy in inputs[:3]:
         copy.wait()
@@ -195,7 +194,7 @@
         def make(i):
             chip = 2 * i + sub
             return chip, remote(
-                ref.at[:, cols(i // groups)], out.at[place, parity], send_x.at[a], recv_x.at[a],
+                ref.at[:, cols(i // groups)], out.at[place, parity], sent.at[0], recv_x.at[a],
                 (chip, base + parity),
             )
 
@@ -205,20 +204,20 @@
         def make(h):
             chip = 2 * (h * groups + my_group) + sub
             return chip, remote(
-                ref.at[:, cols(h)], out.at[slot], send_x.at[a],
-                recv_q.at[slot // block] if a == 2 else recv_x.at[a], (chip, base + parity),
+                ref.at[:, cols(h)], out.at[slot], sent.at[0],
+                recv_q.at[slot // block] if a == 2 else recv_x.at[2], (chip, base + parity),
             )
 
         return make
 
     def forward(a, ref):
-        return remote(ref.at[:, sub], ref.at[:, sub], send_f.at[a], recv_f.at[a], mate)
+        return remote(ref.at[:, sub], ref.at[:, sub], sent.at[0], recv_f.at[a], mate)
 
     def back_query(a, ref, out):
         def make(j):
             c = j * stride + offset
             return c, remote(
-                ref.at[j], out.at[:, cols(my_head)], send_h.at[a], recv_o.at[a], (c, source_tp)
+                ref.at[j], out.at[:, cols(my_head)], sent.at[0], recv_o.at[a], (c, source_tp)
             )
 
         return make
@@ -226,17 +225,26 @@
     def back_block(i):
         c = 2 * i + sub
         return c, remote(
-            dkv.at[:, i, sub], dkv_in.at[:, my_group, :, cols(my_head)], send_h.at[2],
+            dkv.at[:, i, sub], dkv_in.at[:, my_group, :, cols(my_head)], sent.at[0],
             recv_b.at[my_head // per], (c, source_tp),
         )
 
     send_g, send_q = send_query(3, d_ref, gb), send_query(2, own3.at[0], qb)
     send_k, send_v = send_block(0, own3.at[1], kb), send_block(1, own3.at[2], vb)
-    heard(1)
-    inputs[4].wait()
+    upper = me >= n // 2
+    lower = jnp.logical_not(upper)
     early = chunks // 2
-    for s in range(early):
-        start_each(order(s) * per, order(s) * per + per, send_g)
+
+    def send_gradients(places):
+        for s in places:
+            start_each(order(s) * per, order(s) * per + per, send_g)
+
+    @pl.when(upper)
+    def _():
+        heard(1)
+        inputs[4].wait()
+        send_gradients(range(early))
+
     lane = lax.broadcasted_iota(jnp.int32, (1, total), 1)
 
     def number_keys(c, ids):
@@ -258,6 +266,8 @@
                 own3[j, :, span] = jnp.dot(
                     pooled[...], wbuf[j, :, span], preferred_element_type=f32
                 ).astype(bf)
+                if j == 1 and s == 0:
+                    pl.when(lower)(functools.partial(heard, 1))
                 each_head = per if j == 0 else per * groups
                 start_each(order(s) * each_head, (order(s) + 1) * each_head, makers[j])
 
@@ -266,8 +276,13 @@
     project(((1, far_first), (2, far_first)))
     pl.when(outer)(lambda: project(((0, far_first),)))
     pl.when(jnp.logical_not(outer))(lambda: project(((0, far_first[::-1]),)))
-    for s in range(early, chunks):
-        start_each(order(s) * per, order(s) * per + per, send_g)
+
+    @pl.when(lower)
+    def _():
+        inputs[4].wait()
+        send_gradients(range(early))
+
+    send_gradients(range(early, chunks))
 
     @pl.when(parity == sub)
     def _():
@@ -302,7 +317,7 @@
 
         each(lo // 2, hi // 2, act)
         span = pl.ds(lo // 2, (hi - lo) // 2)
-        remote(dkv.at[:, span, 1 - sub], xkv.at[:, span], send_m.at[step], recv_m.at[step], mate).start()
+        remote(dkv.at[:, span, 1 - sub], xkv.at[:, span], sent.at[0], recv_m.at[step], mate).start()
 
     def send_home(step, lo, hi):
         came_in(recv_m.at[step], hi - lo)
@@ -321,23 +336,25 @@
     but_own(came_in, recv_x.at[1], pairs)
     forward(1, vb).start()
     came_in(recv_f.at[0], pairs)
-    came_in(recv_f.at[1], pairs)
-
-    def attend(b):
+
+    def weigh(b):
         lo, reach = b * block, reach_of(b)
         keys = reach * rows
         q = qb[pl.ds(lo, block)].reshape(block * rows, HD)
         k = kb[pl.ds(0, reach // 2)].reshape(keys, HD)
-        v = vb[pl.ds(0, reach // 2)].reshape(keys, HD)
         qid = jnp.concatenate([numbers((lo + j) * stride + offset, row) for j in range(block)], axis=0)
         allowed = qid >= kid[:, :keys]
         score = lax.dot_general(q, k, over_last, preferred_element_type=f32) * scale
         score = jnp.where(allowed, score, -jnp.inf)
         top = jnp.max(score, axis=1, keepdims=True)
         e = jnp.exp(score - top)
-        prob = e * (1.0 / jnp.sum(e, axis=1, keepdims=True))
-        pa[b, :, pl.ds(0, keys)] = prob
-        out = jnp.dot(prob.astype(bf), v, preferred_element_type=f32).astype(bf)
+        pa[b, :, pl.ds(0, keys)] = e * (1.0 / jnp.sum(e, axis=1, keepdims=True))
+
+    def attend(b):
+        lo = b * block
+        keys = reach_of(b) * rows
+        v = vb[pl.ds(0, reach_of(b) // 2)].reshape(keys, HD)
+        out = jnp.dot(pa[b, :, pl.ds(0, keys)].astype(bf), v, preferred_element_type=f32).astype(bf)
         ob[pl.ds(lo, block)] = out.reshape(block, rows, HD)
 
     def differentiate(b, filled):
@@ -373,8 +390,7 @@
     whole = [(i, lo, hi) for i, (lo, hi) in enumerate(((0, middle), (middle, n))) if hi > lo]
     falling = (steps, {b: [(b, reach_of(b - 1), reach_of(b))] for b in steps if reach_of(b) > reach_of(b - 1)})
     rising = (steps[::-1], {steps[0]: whole})
-    upper = me >= n // 2
-    halves = [(upper, rising), (jnp.logical_not(upper), falling)] if len(steps) > 1 else [(me >= 0, falling)]
+    halves = [(upper, rising), (lower, falling)] if len(steps) > 1 else [(me >= 0, falling)]
 
     def work(blocks, spans):
         lead, first = max(1, len(blocks) // 2), blocks[:1]
@@ -384,10 +400,14 @@
                 pl.when(mine_too)(lambda: came_in(recv_q.at[b], block - 1))
                 pl.when(jnp.logical_not(mine_too))(lambda: came_in(recv_q.at[b], block))
             for b in part_of:
+                weigh(b)
+            if part_of is first:
+                came_in(recv_f.at[1], pairs)
+            for b in part_of:
                 attend(b)
             for b in part_of:
                 start_each(b * block, (b + 1) * block, back_o)
-        but_own(came_in, recv_x.at[3], heads)
+        but_own(came_in, recv_x.at[2], heads)
         late, filled = [], 0
         for part_of in (blocks[:lead], blocks[lead:]):
             for b in part_of:
@@ -464,20 +484,7 @@
     sizes = jnp.maximum(jnp.sum(chooser, axis=1, keepdims=True), 1.0)
     pl.when(has_left)(to_left.wait_send)
     pl.when(has_right)(to_right.wait_send)
-    for a in range(2):
-        but_own(went_out, send_x.at[a], pairs)
-        but_own(went_out, send_x.at[2 + a], heads)
-        but_own(went_out, send_h.at[a], heads)
-        went_out(send_f.at[a], pairs)
-
-    def handed_over(blocks, spans):
-        for b in blocks:
-            for i, lo, hi in spans.get(b, ()):
-                went_out(send_m.at[i], hi - lo)
-
-    but_own(went_out, send_h.at[2], 2 * pairs, 2)
-    for here, plan_of in halves:
-        pl.when(here)(functools.partial(handed_over, *plan_of))
+    but_own(went_out, sent.at[0], 8 * pairs + 4 * heads, 8)
     others = own_part.at[pl.ds(0, tp - 1)]
     for here, a, ref in ((has_right, 0, hi_part), (has_left, 1, lo_part)):
         pl.when(here)(lambda: remote(ref, ref, send_r.at[a], recv_r.at[a], mate).wait_recv())
@@ -545,9 +552,10 @@
             pltpu.VMEM((2, groups, rows, feats), bf),
             pltpu.VMEM((tp, rows, width), bf), pltpu.VMEM((tp, rows, width), bf),
             pltpu.VMEM((tp, half, width), bf), pltpu.VMEM((tp, half, width), bf),
-            pltpu.VMEM((max(n, per + 2 * per * groups), rows, HD), bf),
-            dma((5,)), dma((3,)), dma((2,)), dma((2,)), dma((4,)), dma((4,)), dma((steps,)), dma((2,)), dma((2,)),
-            dma((max(2, steps),)), dma((max(2, steps),)), dma((4,)), dma((2,)), dma((heads // per,)), dma((3,)), dma((3,)), pltpu.SemaphoreType.REGULAR((2,)),
+            pltpu.VMEM((8 * pairs + 4 * heads, rows, HD), bf),
+            dma((5,)), dma((3,)), dma((2,)), dma((2,)), dma((1,)), dma((3,)), dma((steps,)), dma((2,)),
+            dma((max(2, steps),)), dma((2,)), dma((heads // per,)), dma((3,)), dma((3,)),
+            pltpu.SemaphoreType.REGULAR((2,)),
         ],
         compiler_params=pltpu.CompilerParams(
             collective_id=0, has_side_effects=True, vmem_limit_bytes=60 << 20

time: 40.6 us -> 40.3 us (level)
  Pallas kernels: 39.7 us -> 39.1 us
    pallas_call x1, Pallas kernels: 38.9 us -> 38.4 us  [shards(): pl.pallas_call(functools.partial(whole_kernel, n, tp, heads, rows, block,...]
where the time goes in v6:
time: 40.3 us; the launch traced here: 39.8 us
  Pallas kernels  39.1 us (97%)
  between operations  0.64 us (2%)
    pallas_call x1, Pallas kernels, shards(): pl.pallas_call(functools.partial(whole_kernel, n, tp, heads, rows, block,...  38.4 us

profile of v6, /device:TPU:0, one launch (start us, length us, event | category | flops | bytes accessed | tf_op | source)
XLA Modules:
  0.0 39.8 jit_solution(7404250456491001191)
XLA Ops:
  0.6 38.4 %whole.1 = (bf16[64,1024]{1,0:T(8,128)(2,1)S(1)}, bf16[256,512]{1,0:T(8,128)(2,1)S(1)}) custom-call(bf16[256,1024]{1,0:T(8,128)(2,1)} %bytes_hbm.1, s32[1,256]{1,0:T(1,128)} %bitcast.1, s32[16]{0:T(128)} %first_hbm.1, s32[2,16]{1,0:T(2,128)} %moved_hbm.1, bf16[3,1024,1024]{2,1,0:T(8,128)(2,1)} %w_hbm.1, bf16[64,1024]{1,0:T(8,128)(2,1)} %d_hbm.1), custom_call_target="tpu_custom_call" | custom-call | tf_op jit(solution)/shard_map/whole/pallas_call | solution.py:534
  39.0 0.8 %emit.1 = (bf16[64,1024]{1,0:T(8,128)(2,1)}, bf16[256,512]{1,0:T(8,128)(2,1)}) custom-call(bf16[64,1024]{1,0:T(8,128)(2,1)S(1)} %get-tuple-element.4.a_ref, bf16[256,512]{1,0:T(8,128)(2,1)S(1)} %get-tuple-element.5.g_ref), custom_call_target="tpu_custom_call" | custom-call | tf_op jit(solution)/shard_map/emit/pallas_call | solution.py:566

commit v7 on v6

--- a/solution.py
+++ b/solution.py
@@ -32,7 +32,7 @@
     bytes_hbm, pob_hbm, first_hbm, moved_hbm, w_hbm, d_hbm,
     attn_ref, grad_ref,
     bytes_ref, pob_ref, first_ref, moved_ref, wbuf, d_ref,
-    blk, came, pooled, own3, qb, gb, kb, vb, pa, ob, dqb, dkv, xkv, dkva,
+    blk, came, pooled, own3, qb, gb, kb, vb, pa, ob, dqb, dkv, xkv, dkva, wt,
     o_in, dq_in, dkv_in, part, own_part, lo_part, hi_part, tally,
     in_sem, w_sem, send_nb, recv_nb, sent, recv_x, recv_q, recv_f, recv_m, recv_o, recv_b, send_r, recv_r, word,
 ):
@@ -258,9 +258,11 @@
     mine = cols(my_head)
     makers = (send_q, send_k, send_v)
 
+    for j in (1, 2, 0):
+        loads[j].wait()
+
     def project(kinds):
         for j, places in kinds:
-            loads[j].wait()
             for s in places:
                 span = cols(order(s) * per, per)
                 own3[j, :, span] = jnp.dot(
@@ -273,9 +275,10 @@
 
     outer = (me < n // 4) | (me >= n - n // 4)
     far_first = list(range(chunks))
-    project(((1, far_first), (2, far_first)))
-    pl.when(outer)(lambda: project(((0, far_first),)))
-    pl.when(jnp.logical_not(outer))(lambda: project(((0, far_first[::-1]),)))
+    distant, close = far_first[:early], far_first[early:]
+    project(((1, distant), (2, distant)))
+    pl.when(outer)(lambda: project(((0, distant), (1, close), (2, close), (0, close))))
+    pl.when(jnp.logical_not(outer))(lambda: project(((1, close), (2, close), (0, close), (0, distant))))
 
     @pl.when(lower)
     def _():
@@ -333,6 +336,8 @@
     steps = list(reversed(range(heads // block)))
     but_own(came_in, recv_x.at[0], pairs)
     forward(0, kb).start()
+    for j in (1, 2):
+        wt[j - 1] = wbuf[j].T
     but_own(came_in, recv_x.at[1], pairs)
     forward(1, vb).start()
     came_in(recv_f.at[0], pairs)
@@ -452,7 +457,7 @@
                 for i in range(1, groups):
                     summed = summed + dkv_in[j - 1, i, :, span].astype(f32)
                 summed = summed.astype(bf)
-            partial += lax.dot_general(summed, wbuf[j, :, span], over_last, preferred_element_type=f32)
+            partial += jnp.dot(summed, wt[j - 1, span], preferred_element_type=f32)
     for t in range(tp):
         part[t] = partial[:, t * width : (t + 1) * width].astype(bf)
     edge_lo, edge_hi = pl.ds(0, half), pl.ds(rows - half, half)
@@ -547,7 +552,7 @@
             pltpu.VMEM((steps, block * rows, total), f32),
             pltpu.VMEM((heads, rows, HD), bf), pltpu.VMEM((heads, rows, HD), bf),
             pltpu.VMEM((2, pairs, 2, rows, HD), bf), pltpu.VMEM((2, pairs, rows, HD), bf),
-            pltpu.VMEM((total, 2 * HD), f32),
+            pltpu.VMEM((total, 2 * HD), f32), pltpu.VMEM((2, feats, model), bf),
             pltpu.VMEM((rows, feats), bf), pltpu.VMEM((rows, feats), bf),
             pltpu.VMEM((2, groups, rows, feats), bf),
             pltpu.VMEM((tp, rows, width), bf), pltpu.VMEM((tp, rows, width), bf),

time: 40.3 us -> 39.5 us (0.980)
  Pallas kernels: 39.1 us -> 38.4 us
    pallas_call x1, Pallas kernels: 38.4 us -> 37.7 us  [shards(): pl.pallas_call(functools.partial(whole_kernel, n, tp, heads, rows, block,...]
where the time goes in v7:
time: 39.5 us; the launch traced here: 39.1 us
  Pallas kernels  38.4 us (97%)
  between operations  0.64 us (2%)
    pallas_call x1, Pallas kernels, shards(): pl.pallas_call(functools.partial(whole_kernel, n, tp, heads, rows, block,...  37.7 us

profile of v7, /device:TPU:0, one launch (start us, length us, event | category | flops | bytes accessed | tf_op | source)
XLA Modules:
  0.0 39.1 jit_solution(2887718418262996362)
XLA Ops:
  0.6 37.7 %whole.1 = (bf16[64,1024]{1,0:T(8,128)(2,1)S(1)}, bf16[256,512]{1,0:T(8,128)(2,1)S(1)}) custom-call(bf16[256,1024]{1,0:T(8,128)(2,1)} %bytes_hbm.1, s32[1,256]{1,0:T(1,128)} %bitcast.1, s32[16]{0:T(128)} %first_hbm.1, s32[2,16]{1,0:T(2,128)} %moved_hbm.1, bf16[3,1024,1024]{2,1,0:T(8,128)(2,1)} %w_hbm.1, bf16[64,1024]{1,0:T(8,128)(2,1)} %d_hbm.1), custom_call_target="tpu_custom_call" | custom-call | tf_op jit(solution)/shard_map/whole/pallas_call | solution.py:539
  38.3 0.8 %emit.1 = (bf16[64,1024]{1,0:T(8,128)(2,1)}, bf16[256,512]{1,0:T(8,128)(2,1)}) custom-call(bf16[64,1024]{1,0:T(8,128)(2,1)S(1)} %get-tuple-element.4.a_ref, bf16[256,512]{1,0:T(8,128)(2,1)S(1)} %get-tuple-element.5.g_ref), custom_call_target="tpu_custom_call" | custom-call | tf_op jit(solution)/shard_map/emit/pallas_call | solution.py:571

commit v8 on v7

--- a/solution.py
+++ b/solution.py
@@ -72,6 +72,11 @@
         back = chunks - 1 - s
         return upper * mid + lax.rem(here + back, mid)
 
+    size = bytes_ref.shape[0]
+    pieces = 4 if size % 64 == 0 else 1
+    for i in range(pieces):
+        piece = pl.ds(i * (size // pieces), size // pieces)
+        pltpu.make_async_copy(bytes_hbm.at[piece], bytes_ref.at[piece], in_sem.at[3]).start()
     inputs = [
         pltpu.make_async_copy(src, dst, in_sem.at[i])
         for i, (src, dst) in enumerate((
@@ -79,7 +84,7 @@
             (d_hbm, d_ref),
         ))
     ]
-    for copy in inputs:
+    for copy in inputs[:3] + inputs[4:]:
         copy.start()
     barrier = pltpu.get_barrier_semaphore()
 
@@ -399,7 +404,7 @@
 
     def work(blocks, spans):
         lead, first = max(1, len(blocks) // 2), blocks[:1]
-        for part_of in (first, blocks[1:]):
+        for part_of in (first, blocks[1:lead], blocks[lead:]):
             for b in part_of:
                 mine_too = at_home & (slot // block == b)
                 pl.when(mine_too)(lambda: came_in(recv_q.at[b], block - 1))

time: 39.5 us -> 39.3 us (level)
  no operation moved by 1% of the time
where the time goes in v8:
time: 39.3 us; the launch traced here: 38.8 us
  Pallas kernels  38.2 us (97%)
  between operations  0.64 us (2%)
    pallas_call x1, Pallas kernels, shards(): pl.pallas_call(functools.partial(whole_kernel, n, tp, heads, rows, block,...  37.4 us

profile of v8, /device:TPU:0, one launch (start us, length us, event | category | flops | bytes accessed | tf_op | source)
XLA Modules:
  0.0 38.8 jit_solution(12487595308397835555)
XLA Ops:
  0.6 37.4 %whole.1 = (bf16[64,1024]{1,0:T(8,128)(2,1)S(1)}, bf16[256,512]{1,0:T(8,128)(2,1)S(1)}) custom-call(bf16[256,1024]{1,0:T(8,128)(2,1)} %bytes_hbm.1, s32[1,256]{1,0:T(1,128)} %bitcast.1, s32[16]{0:T(128)} %first_hbm.1, s32[2,16]{1,0:T(2,128)} %moved_hbm.1, bf16[3,1024,1024]{2,1,0:T(8,128)(2,1)} %w_hbm.1, bf16[64,1024]{1,0:T(8,128)(2,1)} %d_hbm.1), custom_call_target="tpu_custom_call" | custom-call | tf_op jit(solution)/shard_map/whole/pallas_call | solution.py:544
  38.1 0.8 %emit.1 = (bf16[64,1024]{1,0:T(8,128)(2,1)}, bf16[256,512]{1,0:T(8,128)(2,1)}) custom-call(bf16[64,1024]{1,0:T(8,128)(2,1)S(1)} %get-tuple-element.4.a_ref, bf16[256,512]{1,0:T(8,128)(2,1)S(1)} %get-tuple-element.5.g_ref), custom_call_target="tpu_custom_call" | custom-call | tf_op jit(solution)/shard_map/emit/pallas_call | solution.py:576
